TPU v7x, 256 devices: a whole 4x4x8 slice. The times are simulated.
256 devices in a mesh: dp: 4 (over y), tensor: 8 (over z), pipe: 8 (over x, core).
Axes of the slice: x: 4, y: 4, z: 8, core: 2. Of those that a mesh axis runs over, the one named last changes fastest.
Arguments:
- acts: bfloat16 [24576, 4096], P(('dp', 'pipe')), may hold values from -6 to 6
- grad_hidden: bfloat16 [24576, 14336], P(('dp', 'pipe'), 'tensor'), may hold values from -384 to 384
- token_count: int32 [32], P(('dp', 'pipe')), may hold values from 1 to 768, as said below
- hot_ids: int32 [8, 179], P('tensor'), may hold values from 0 to 1791, as said below
- block_owner: int32 [112, 1], P('tensor'), may hold values from 0 to 7; in each aligned block of 14 rows (0 to 13, 14 to 27, ...) at most 4 rows name the same one
- master_hot: float32 [1432, 4096], P('tensor', ('dp', 'pipe')), may hold values from -6 to 6
- moment_hot: float32 [1432, 4096], P('tensor', ('dp', 'pipe')), may hold values from -3 to 3
- second_hot: float32 [1432, 4096], P('tensor', ('dp', 'pipe')), may hold values from 0.1 to 100
Outputs:
- new_master: float32 [1432, 4096], P('tensor', ('dp', 'pipe'))
- new_moment: float32 [1432, 4096], P('tensor', ('dp', 'pipe'))
- new_second: float32 [1432, 4096], P('tensor', ('dp', 'pipe'))
- hot_weights: bfloat16 [1432, 4096], P('tensor', 'dp')
- cold_sectioning: bfloat16 [256, 4096, 128], P('tensor', ('dp', 'pipe'))
Inputs may be any that keep to these rules, and one draw needn't show every extreme that they name: `token_count`: each micro-batch has at least one live token, and some micro-batch has exactly 768. `hot_ids`: each row lists 179 different offsets. `block_owner`: within the 14 blocks of one tensor index, no owner is named more than 4 times.
All inputs are finite; a program needn't handle non-finite values.
Results may differ from a plain program's by a relative error of at most 0.015.
Values may be sent and summed in bfloat16 or wider, within the bound.
No kernel may reach another device: no remote copies, remote signals or barrier semaphores. Data moves between devices by JAX's collectives and lax.ppermute only.
A program may use at most 128 MiB of HBM per device.

v0:
```python
import functools

import jax
import jax.numpy as jnp
from jax import lax
from jax.experimental import pallas as pl
from jax.experimental.pallas import tpu as pltpu
from jax.sharding import Mesh
from jax.sharding import PartitionSpec as P


CB = 128
DP_PIPE = ("dp", "pipe_0", "pipe_1")
SLOTS = 4
COLOURS = ((0, 4), (4, 4), (8, 3), (11, 3))
SPARE = 16
EVEN = [(0, 1), (1, 0), (2, 3), (3, 2)]
ODD = [(1, 2), (2, 1), (3, 0), (0, 3)]
DIMS = (("pipe_0", EVEN), ("dp", EVEN), ("pipe_0", ODD), ("dp", ODD))
SWAP = [(0, 1), (1, 0)]
ORDERS = ((0, 1, 2, 3), (1, 2, 3, 0), (2, 3, 0, 1), (3, 0, 1, 2))
MiB = 1 << 20


def gray(p):
    return p ^ (p >> 1)


def dest_block(k, half, own, q):
    idx = half * 8 + q
    rx = ry = 0
    for s in range(4):
        bit = (idx >> (3 - s)) & 1
        d = ORDERS[k][s]
        if d % 2 == 0:
            rx |= bit << (d // 2)
        else:
            ry |= bit << (d // 2)
    return far(lax.axis_index("dp"), ry) * 8 + pipe_block(rx, 1 - own)


def far(p, r):
    return gray(gray(p) ^ r)


def pipe_block(rx, rc):
    return far(lax.axis_index("pipe_0"), rx) * 2 + (lax.axis_index("pipe_1") ^ rc)


def load_kernel(cnt_ref, a_hbm, g_hbm, a_ref, l0, l1, l2, l3, stage, a_sem, g_sem):
    toks = stage.shape[1]
    g_copies = [
        pltpu.make_async_copy(
            g_hbm.at[:, first * CB : (first + n) * CB],
            stage.at[k, :, : n * CB],
            g_sem.at[k],
        )
        for k, (first, n) in enumerate(COLOURS)
    ]
    a_copy = pltpu.make_async_copy(a_hbm, a_ref, a_sem)
    for cp in g_copies:
        cp.start()
    a_copy.start()
    live = lax.broadcasted_iota(jnp.int32, (toks, CB), 0) < cnt_ref[0]
    for k, ((first, n), out) in enumerate(zip(COLOURS, (l0, l1, l2, l3))):
        g_copies[k].wait()
        for i in range(n):
            v = stage[k, :, i * CB : (i + 1) * CB]
            out[i * CB : (i + 1) * CB, :] = jnp.where(live, v, jnp.zeros_like(v)).T
    a_copy.wait()


VM = pl.BlockSpec(memory_space=pltpu.VMEM)
HB = pl.BlockSpec(memory_space=pltpu.HBM)


def loaded(cnt, acts, grad_hidden):
    toks = acts.shape[0]
    outs = [jax.ShapeDtypeStruct(acts.shape, acts.dtype)]
    outs += [jax.ShapeDtypeStruct((n * CB, toks), jnp.bfloat16) for _, n in COLOURS]
    return pl.pallas_call(
        load_kernel,
        grid_spec=pltpu.PrefetchScalarGridSpec(
            num_scalar_prefetch=1,
            grid=(),
            in_specs=[HB, HB],
            out_specs=[VM] * 5,
            scratch_shapes=[
                pltpu.VMEM((4, toks, 4 * CB), jnp.bfloat16),
                pltpu.SemaphoreType.DMA,
                pltpu.SemaphoreType.DMA((4,)),
            ],
        ),
        out_shape=outs,
        compiler_params=pltpu.CompilerParams(vmem_limit_bytes=16 * MiB),
        cost_estimate=pl.CostEstimate(flops=2000000000, bytes_accessed=0, transcendentals=0),
        name="load",
    )(
        cnt,
        pltpu.with_memory_space_constraint(acts, pltpu.HBM),
        pltpu.with_memory_space_constraint(grad_hidden, pltpu.HBM),
    )


def mm_kernel(cnt_ref, l_ref, a_ref, *outs, spare, k, half, owns):
    n = l_ref.shape[0]
    left = l_ref
    for o_ref, own in zip(outs, owns):

        def pair(i, _, o_ref=o_ref, own=own):
            blk = [
                a_ref[:, pl.ds(pl.multiple_of(dest_block(k, half, own, 2 * i + j) * CB, CB), CB)]
                for j in range(2)
            ]
            r = jnp.dot(
                left[...], jnp.concatenate(blk, axis=1), preferred_element_type=jnp.float32
            ).astype(jnp.bfloat16)
            o_ref[2 * i, :n, :] = r[:, :CB]
            o_ref[2 * i + 1, :n, :] = r[:, CB:]
            return 0

        lax.fori_loop(0, 4, pair, 0, unroll=4 if half else 2)
        if spare:
            c = cnt_ref[0]
            row = lax.broadcasted_iota(jnp.int32, (SPARE, CB), 0)
            digit = jnp.where(
                row == 0, c & 7, jnp.where(row == 1, (c >> 3) & 7, jnp.where(row == 2, c >> 6, 0))
            )
            digit = digit.astype(jnp.float32).astype(jnp.bfloat16)
            for i in range(8):
                o_ref[i, n:, :] = digit


def product(cnt, left, acts, k, half, owns):
    toks = acts.shape[0]
    n = left.shape[0]
    spare = SPARE if k == 3 else 0
    return pl.pallas_call(
        functools.partial(mm_kernel, spare=spare, k=k, half=half, owns=owns),
        grid_spec=pltpu.PrefetchScalarGridSpec(
            num_scalar_prefetch=1,
            grid=(),
            in_specs=[VM, VM],
            out_specs=[VM] * len(owns),
        ),
        out_shape=[jax.ShapeDtypeStruct((8, n + spare, CB), jnp.bfloat16)] * len(owns),
        compiler_params=pltpu.CompilerParams(vmem_limit_bytes=8 * MiB),
        cost_estimate=pl.CostEstimate(
            flops=2 * 8 * CB * n * toks * len(owns), bytes_accessed=0, transcendentals=0
        ),
        name="mm",
    )(cnt, left, acts)


PACKS = {d: ((d, 0, SLOTS),) for d in range(8)}


def tail_kernel(ids_ref, own_ref, g0, g1, g2, g3, hot_ref, *refs):
    z_refs, acc, pack = refs[:8], refs[8], refs[9]
    for (first, nblk), g in zip(COLOURS, (g0, g1, g2, g3)):
        acc[first * CB : (first + nblk) * CB, :] = g[: nblk * CB, :]
    digits = g3[COLOURS[3][1] * CB : COLOURS[3][1] * CB + 8, :]
    total = digits[0:1, :] + 8.0 * digits[1:2, :] + 64.0 * digits[2:3, :]
    pack[...] = jnp.zeros_like(pack)

    def take(i, _):
        h = ids_ref[0, i]
        hot_ref[pl.ds(i, 1), :] = acc[pl.ds(h, 1), :] / total
        acc[pl.ds(h, 1), :] = jnp.zeros((1, CB), jnp.float32)
        return 0

    lax.fori_loop(0, hot_ref.shape[0], take, 0, unroll=4)
    for b in range(acc.shape[0] // CB):
        x = acc[b * CB : (b + 1) * CB, :] / total
        owner = own_ref[b]
        slot = jnp.int32(0)
        for e in range(b):
            slot += (own_ref[e] == owner).astype(jnp.int32)
        pack[((owner - lax.axis_index("tensor")) & 7) * SLOTS + slot] = x.T.astype(jnp.bfloat16)
    for d in range(8):
        at = 0
        for e, lo, n in PACKS[d]:
            z_refs[d][at : at + n] = pack[e * SLOTS + lo : e * SLOTS + lo + n]
            at += n


def tail(ids, owners, gs, count):
    outs = [jax.ShapeDtypeStruct((count, CB), jnp.float32)]
    for d in range(8):
        outs.append(jax.ShapeDtypeStruct((sum(p[2] for p in PACKS[d]), CB, CB), jnp.bfloat16))
    return pl.pallas_call(
        tail_kernel,
        grid_spec=pltpu.PrefetchScalarGridSpec(
            num_scalar_prefetch=2,
            grid=(),
            in_specs=[VM] * 4,
            out_specs=[VM] * 9,
            scratch_shapes=[
                pltpu.VMEM((14 * CB, CB), jnp.float32),
                pltpu.VMEM((8 * SLOTS, CB, CB), jnp.bfloat16),
            ],
        ),
        out_shape=outs,
        compiler_params=pltpu.CompilerParams(vmem_limit_bytes=24 * MiB),
        name="tail",
    )(ids, owners, *gs)


def adam_kernel(g_ref, ma_ref, mo_ref, se_ref, nma_ref, nmo_ref, nse_ref, hw_ref):
    g_hot = g_ref[...]
    mo = 0.9 * mo_ref[...] + 0.1 * g_hot
    se = 0.95 * se_ref[...] + 0.05 * g_hot * g_hot
    bias_one = 1.0 - 0.9**4
    bias_two = 1.0 - 0.95**4
    ma = ma_ref[...] - 0.02 * (mo / bias_one) / (jnp.sqrt(se / bias_two) + 1e-08)
    nmo_ref[...] = mo
    nse_ref[...] = se
    nma_ref[...] = ma
    hw_ref[...] = ma.astype(jnp.bfloat16)


def adam(g_hot, master, moment, second):
    f32 = jax.ShapeDtypeStruct(master.shape, jnp.float32)
    return pl.pallas_call(
        adam_kernel,
        in_specs=[VM] * 4,
        out_specs=[VM] * 4,
        out_shape=[f32, f32, f32, jax.ShapeDtypeStruct(master.shape, jnp.bfloat16)],
        compiler_params=pltpu.CompilerParams(vmem_limit_bytes=8 * MiB),
        name="adam",
    )(g_hot, master, moment, second)


PLACES = tuple((d, 0, SLOTS) for d in range(8))


def join_kernel(a_ref, b_ref, c_ref, d_ref, *refs):
    z_refs, o_ref, cold_ref, sem = refs[:8], refs[8], refs[9], refs[10]
    z = lax.axis_index("tensor")
    copies = []
    for i, (d, lo, n) in enumerate(PLACES):
        at = ((z - d) & 7) * SLOTS + lo
        copies.append(
            pltpu.make_async_copy(z_refs[i].at[0:n], cold_ref.at[pl.ds(at, n)], sem.at[i])
        )
    for cp in copies:
        cp.start()
    for r, piece in enumerate(
        (a_ref[...], b_ref[...], c_ref[0], c_ref[1], d_ref[0], d_ref[1], d_ref[2], d_ref[3])
    ):
        o_ref[:, pl.ds(pl.multiple_of(pipe_block(r >> 1, r & 1) * CB, CB), CB)] = piece
    for cp in copies:
        cp.wait()


def joined(a, b, c, d, recv):
    return pl.pallas_call(
        join_kernel,
        in_specs=[VM] * 12,
        out_specs=[VM, HB],
        scratch_shapes=[pltpu.SemaphoreType.DMA((8,))],
        out_shape=[
            jax.ShapeDtypeStruct((a.shape[0], 8 * CB), a.dtype),
            jax.ShapeDtypeStruct((8 * SLOTS, CB, CB), jnp.bfloat16),
        ],
        compiler_params=pltpu.CompilerParams(vmem_limit_bytes=8 * MiB),
        name="join",
    )(a, b, c, d, *recv)


def wide(*xs):
    out = xs[0].astype(jnp.float32)
    for x in xs[1:]:
        out = out + x.astype(jnp.float32)
    return out


def shards(
    acts, grad_hidden, token_count, hot_ids, block_owner, master_hot, moment_hot, second_hot
):
    acts_v, *left = loaded(token_count, acts, grad_hidden)

    def mm(k, half, owns):
        return product(token_count, left[k], acts_v, k, half, owns)

    def moved(v, axis, pairs):
        return lax.ppermute(v, axis, pairs)

    def summed(*xs):
        return wide(*xs).astype(jnp.bfloat16)

    first = []
    for k in range(4):
        (peer,) = mm(k, 1, (0,))
        got = moved(peer, "pipe_1", SWAP)
        (mine,) = mm(k, 1, (1,))
        first.append(moved(summed(mine, got), *DIMS[ORDERS[k][0]]))
    parts = []
    for k in range(4):
        peer, mine = mm(k, 0, (0, 1))
        parts.append([mine, moved(peer, "pipe_1", SWAP), first[k]])
    size = 8
    for s in range(1, 4):
        half = size // 2
        for k in range(4):
            send = summed(*[p[half:size] for p in parts[k]])
            parts[k].append(moved(send, *DIMS[ORDERS[k][s]]))
        size = half
    gs = []
    for k in range(4):
        gs.append(wide(*[p[0] for p in parts[k]]))
    g_hot, *packs = tail(hot_ids, block_owner[:, 0], gs, hot_ids.shape[1])
    new_master, new_moment, new_second, hw = adam(g_hot, master_hot, moment_hot, second_hot)
    recv = [packs[0]]
    for d in range(1, 8):
        recv.append(moved(packs[d], "tensor", [(i, (i + d) % 8) for i in range(8)]))
    hw_b = moved(hw, "pipe_1", SWAP)
    two = jnp.stack([hw, hw_b])
    hw_c = moved(two, "pipe_0", EVEN)
    hw_d = moved(jnp.concatenate([two, hw_c]), "pipe_0", ODD)
    hot_weights, cold = joined(hw, hw_b, hw_c, hw_d, recv)
    return (new_master, new_moment, new_second, hot_weights, cold)


def solution(mesh):
    split = Mesh(
        mesh.devices.reshape(mesh.shape["dp"], mesh.shape["tensor"], 4, 2),
        ("dp", "tensor", "pipe_0", "pipe_1"),
    )
    return jax.shard_map(
        shards,
        mesh=split,
        in_specs=(
            P(DP_PIPE, None),
            P(DP_PIPE, "tensor"),
            P(DP_PIPE),
            P("tensor", None),
            P("tensor", None),
            P("tensor", DP_PIPE),
            P("tensor", DP_PIPE),
            P("tensor", DP_PIPE),
        ),
        out_specs=(
            P("tensor", DP_PIPE),
            P("tensor", DP_PIPE),
            P("tensor", DP_PIPE),
            P("tensor", "dp"),
            P("tensor", DP_PIPE, None),
        ),
        check_vma=False,
    )
```

profile of v0, /device:TPU:1, one launch (start us, length us, event | category | flops | bytes accessed | tf_op | source)
XLA Modules:
  0.0 161.1 jit_solution(6702152006791716153)
XLA Ops:
  1.3 3.7 %load.1 = (bf16[768,4096]{1,0:T(8,128)(2,1)S(1)}, bf16[512,768]{1,0:T(8,128)(2,1)S(1)}, bf16[512,768]{1,0:T(8,128)(2,1)S(1)}, bf16[384,768]{1,0:T(8,128)(2,1)S(1)}, bf16[384,768]{1,0:T(8,128)(2,1)S(1)}) custom-call(s32[1]{0:T(128)S(6)} %copy.13.cnt_ref, bf16[768,4096]{1,0:T(8,128)(2,1)} %a_hbm.1, bf16[768,1792]{1,0:T(8,128)(2,1)} %g_hbm.1), custom_call_target="tpu_custom_call" | custom-call | flops 2000000000 | tf_op jit(solution)/shard_map/load/pallas_call | solution.py:81
  5.0 0.9 mm.20
  5.9 3.3 %collective-permute-start.13 = (bf16[8,384,128]{2,1,0:T(8,128)(2,1)S(1)}, bf16[8,384,128]{2,1,0:T(8,128)(2,1)S(1)}, u32[]{:S(2)}, u32[]{:S(2)}) collective-permute-start(bf16[8,384,128]{2,1,0:T(8,128)(2,1)S(1)} %mm.20), channel_id=1, source_target_pairs={{0,1},{1,0},{2,3},{3,2},{4,5},{5,4},{6,7},{7,6},{8,9},{9,8},{10,11... | collective-permute-start | bytes 2359304 | tf_op jit(solution)/shard_map/ppermute | solution.py:287
  9.2 0.9 mm.23
  10.2 2.2 %mm.18 = (bf16[8,384,128]{2,1,0:T(8,128)(2,1)S(1)}, bf16[8,384,128]{2,1,0:T(8,128)(2,1)S(1)}) custom-call(s32[1]{0:T(128)S(6)} %copy.13.cnt_ref, bf16[384,768]{1,0:T(8,128)(2,1)S(1)} %get-tuple-element.40.l_ref, bf16[768,4096]{1,0:T(8,128)(2,1)S(1)} %get-tuple-element.34.a_ref), custom_call_target="tpu_custom_call" | custom-call | flops 1207959552 | tf_op jit(solution)/shard_map/mm/pallas_call | solution.py:138
  12.4 0.5 collective-permute-start.12
  13.0 1.1 mm.17
  14.2 1.1 mm.14
  15.3 0.7 collective-permute-start.1
  16.0 1.1 mm.16
  17.1 1.1 mm.13
  18.2 0.9 mm.19
  19.1 2.2 %mm.21 = (bf16[8,400,128]{2,1,0:T(8,128)(2,1)S(1)}, bf16[8,400,128]{2,1,0:T(8,128)(2,1)S(1)}) custom-call(s32[1]{0:T(128)S(6)} %copy.13.cnt_ref, bf16[384,768]{1,0:T(8,128)(2,1)S(1)} %get-tuple-element.43.l_ref, bf16[768,4096]{1,0:T(8,128)(2,1)S(1)} %get-tuple-element.34.a_ref), custom_call_target="tpu_custom_call" | custom-call | flops 1207959552 | tf_op jit(solution)/shard_map/mm/pallas_call | solution.py:138
  21.3 2.6 %mm.15 = (bf16[8,512,128]{2,1,0:T(8,128)(2,1)S(1)}, bf16[8,512,128]{2,1,0:T(8,128)(2,1)S(1)}) custom-call(s32[1]{0:T(128)S(6)} %copy.13.cnt_ref, bf16[512,768]{1,0:T(8,128)(2,1)S(1)} %get-tuple-element.37.l_ref, bf16[768,4096]{1,0:T(8,128)(2,1)S(1)} %get-tuple-element.34.a_ref), custom_call_target="tpu_custom_call" | custom-call | flops 1610612736 | tf_op jit(solution)/shard_map/mm/pallas_call | solution.py:138
  24.0 0.2 add_convert_fusion.3
  24.2 0.9 collective-permute-start.14
  25.0 0.9 mm.22
  25.9 2.6 %mm.12 = (bf16[8,512,128]{2,1,0:T(8,128)(2,1)S(1)}, bf16[8,512,128]{2,1,0:T(8,128)(2,1)S(1)}) custom-call(s32[1]{0:T(128)S(6)} %copy.13.cnt_ref, bf16[512,768]{1,0:T(8,128)(2,1)S(1)} %get-tuple-element.33.l_ref, bf16[768,4096]{1,0:T(8,128)(2,1)S(1)} %get-tuple-element.34.a_ref), custom_call_target="tpu_custom_call" | custom-call | flops 1610612736 | tf_op jit(solution)/shard_map/mm/pallas_call | solution.py:138
  28.5 0.4 collective-permute-start.18
  28.9 0.2 add_convert_fusion.2
  29.1 2.8 %collective-permute-start.20 = (bf16[8,400,128]{2,1,0:T(8,128)(2,1)S(1)}, bf16[8,400,128]{2,1,0:T(8,128)(2,1)S(1)}, u32[]{:S(2)}, u32[]{:S(2)}) collective-permute-start(bf16[8,400,128]{2,1,0:T(8,128)(2,1)S(1)} %add_convert_fusion.2), channel_id=1, source_target_pairs={{64,128},{128,64},{192,0},{0,192},{65,129},{129,65},{193,1},{1,193... | collective-permute-start | bytes 2457608 | tf_op jit(solution)/shard_map/ppermute | solution.py:287
  32.0 0.3 add_convert_fusion
  32.3 0.6 collective-permute-start.6
  32.8 11.7 %collective-permute-done.14 = bf16[8,384,128]{2,1,0:T(8,128)(2,1)S(1)} collective-permute-done((bf16[8,384,128]{2,1,0:T(8,128)(2,1)S(1)}, bf16[8,384,128]{2,1,0:T(8,128)(2,1)S(1)}, u32[]{:S(2)}, u32[]{:S(2)}) %collective-permute-start.14) | collective-permute-done | bytes 786464 | tf_op jit(solution)/shard_map/ppermute | solution.py:287
  44.7 1.6 collective-permute-start.15
  46.3 0.3 add_convert_fusion.1
  46.6 1.5 collective-permute-start
  48.1 2.0 %collective-permute-done.20 = bf16[8,400,128]{2,1,0:T(8,128)(2,1)S(1)} collective-permute-done((bf16[8,400,128]{2,1,0:T(8,128)(2,1)S(1)}, bf16[8,400,128]{2,1,0:T(8,128)(2,1)S(1)}, u32[]{:S(2)}, u32[]{:S(2)}) %collective-permute-start.20) | collective-permute-done | bytes 819232 | tf_op jit(solution)/shard_map/ppermute | solution.py:287
  50.2 0.2 add_convert_fusion.6
  50.3 8.3 %collective-permute-done.15 = bf16[4,384,128]{2,1,0:T(8,128)(2,1)S(1)} collective-permute-done((bf16[4,384,128]{2,1,0:T(8,128)(2,1)S(1)}, bf16[4,384,128]{2,1,0:T(8,128)(2,1)S(1)}, u32[]{:S(2)}, u32[]{:S(2)}) %collective-permute-start.15) | collective-permute-done | bytes 393248 | tf_op jit(solution)/shard_map/ppermute | solution.py:287
  58.7 23.3 %collective-permute-done.21 = bf16[4,400,128]{2,1,0:T(8,128)(2,1)S(1)} collective-permute-done((bf16[4,400,128]{2,1,0:T(8,128)(2,1)S(1)}, bf16[4,400,128]{2,1,0:T(8,128)(2,1)S(1)}, u32[]{:S(2)}, u32[]{:S(2)}) %collective-permute-start.21) | collective-permute-done | bytes 409632 | tf_op jit(solution)/shard_map/ppermute | solution.py:287
  82.3 0.2 add_convert_fusion.4
  82.5 2.1 %collective-permute-start.9 = (bf16[4,512,128]{2,1,0:T(8,128)(2,1)S(1)}, bf16[4,512,128]{2,1,0:T(8,128)(2,1)S(1)}, u32[]{:S(2)}, u32[]{:S(2)}) collective-permute-start(bf16[4,512,128]{2,1,0:T(8,128)(2,1)S(1)} %add_convert_fusion.4), channel_id=1, source_target_pairs={{2,4},{4,2},{6,0},{0,6},{3,5},{5,3},{7,1},{1,7},{10,12},{12,10},{1... | collective-permute-start | bytes 1572872 | tf_op jit(solution)/shard_map/ppermute | solution.py:287
  84.6 0.2 add_convert_fusion.5
  84.8 1.5 collective-permute-start.3
  86.3 0.2 collective-permute-done.16
  86.9 2.1 %collective-permute-start.23 = (bf16[1,400,128]{2,1,0:T(8,128)(2,1)S(1)}, bf16[1,400,128]{2,1,0:T(8,128)(2,1)S(1)}, u32[]{:S(2)}, u32[]{:S(2)}) collective-permute-start(bf16[1,400,128]{2,1,0:T(8,128)(2,1)S(1)} %add_convert_fusion.14), channel_id=1, source_target_pairs={{2,4},{4,2},{6,0},{0,6},{3,5},{5,3},{7,1},{1,7},{10,12},{12,10},{1... | collective-permute-start | bytes 307208 | tf_op jit(solution)/shard_map/ppermute | solution.py:287
  89.0 11.3 %collective-permute-done.17 = bf16[1,384,128]{2,1,0:T(8,128)(2,1)S(1)} collective-permute-done((bf16[1,384,128]{2,1,0:T(8,128)(2,1)S(1)}, bf16[1,384,128]{2,1,0:T(8,128)(2,1)S(1)}, u32[]{:S(2)}, u32[]{:S(2)}) %collective-permute-start.17) | collective-permute-done | bytes 98336 | tf_op jit(solution)/shard_map/ppermute | solution.py:287
  100.6 1.5 collective-permute-start.10
  102.3 1.6 collective-permute-start.4
  103.9 3.2 %collective-permute-done.10 = bf16[2,512,128]{2,1,0:T(8,128)(2,1)S(1)} collective-permute-done((bf16[2,512,128]{2,1,0:T(8,128)(2,1)S(1)}, bf16[2,512,128]{2,1,0:T(8,128)(2,1)S(1)}, u32[]{:S(2)}, u32[]{:S(2)}) %collective-permute-start.10) | collective-permute-done | bytes 262176 | tf_op jit(solution)/shard_map/ppermute | solution.py:287
  107.3 0.6 collective-permute-start.11
  107.9 1.2 collective-permute-done.4
  109.2 1.3 collective-permute-start.5
  110.5 0.9 collective-permute-done.11
  111.6 2.8 %collective-permute-done.5 = bf16[1,512,128]{2,1,0:T(8,128)(2,1)S(1)} collective-permute-done((bf16[1,512,128]{2,1,0:T(8,128)(2,1)S(1)}, bf16[1,512,128]{2,1,0:T(8,128)(2,1)S(1)}, u32[]{:S(2)}, u32[]{:S(2)}) %collective-permute-start.5) | collective-permute-done | bytes 131104 | tf_op jit(solution)/shard_map/ppermute | solution.py:287
  114.4 1.7 %tail.1 = (f32[179,128]{1,0:T(8,128)S(1)}, bf16[4,128,128]{2,1,0:T(8,128)(2,1)S(1)}, bf16[4,128,128]{2,1,0:T(8,128)(2,1)S(1)}, bf16[4,128,128]{2,1,0:T(8,128)(2,...) custom-call(s32[1,179]{1,0:T(1,128)S(1)} %copy-done.3, ...), custom_call_target="tpu_custom_call" | custom-call | tf_op jit(solution)/shard_map/tail/pallas_call | solution.py:191
  116.2 0.7 adam.1
  116.9 6.0 %collective-permute-start.24 = (bf16[179,128]{1,0:T(8,128)(2,1)S(1)}, bf16[179,128]{1,0:T(8,128)(2,1)S(1)}, u32[]{:S(2)}, u32[]{:S(2)}) collective-permute-start(bf16[179,128]{1,0:T(8,128)(2,1)S(1)} %get-tuple-element.50.a_ref), channel_id=1, source_target_pairs={{0,1},{1,0},{2,3},{3,2},{4,5},{5,4},{6,7},{7,6},{8,9},{9,8},{10,11... | collective-permute-start | bytes 137480 | tf_op jit(solution)/shard_map/ppermute | solution.py:287
  122.9 0.9 collective-permute-done.24.b_ref
  123.8 0.3 collective-permute-start.25
  124.2 1.6 collective-permute-start.27
  125.8 3.0 %collective-permute-start.28 = (bf16[4,128,128]{2,1,0:T(8,128)(2,1)S(1)}, bf16[4,128,128]{2,1,0:T(8,128)(2,1)S(1)}, u32[]{:S(2)}, u32[]{:S(2)}) collective-permute-start(bf16[4,128,128]{2,1,0:T(8,128)(2,1)S(1)} %get-tuple-element.53), channel_id=1, source_target_pairs={{0,16},{8,24},{16,32},{24,40},{32,48},{40,56},{48,0},{56,8},{1,17}... | collective-permute-start | bytes 393224 | tf_op jit(solution)/shard_map/ppermute | solution.py:287
  128.8 3.8 %collective-permute-start.29 = (bf16[4,128,128]{2,1,0:T(8,128)(2,1)S(1)}, bf16[4,128,128]{2,1,0:T(8,128)(2,1)S(1)}, u32[]{:S(2)}, u32[]{:S(2)}) collective-permute-start(bf16[4,128,128]{2,1,0:T(8,128)(2,1)S(1)} %get-tuple-element.54), channel_id=1, source_target_pairs={{0,24},{8,32},{16,40},{24,48},{32,56},{40,0},{48,8},{56,16},{1,25}... | collective-permute-start | bytes 393224 | tf_op jit(solution)/shard_map/ppermute | solution.py:287
  132.5 1.1 collective-permute-start.26
  133.6 2.4 %collective-permute-start.30 = (bf16[4,128,128]{2,1,0:T(8,128)(2,1)S(1)}, bf16[4,128,128]{2,1,0:T(8,128)(2,1)S(1)}, u32[]{:S(2)}, u32[]{:S(2)}) collective-permute-start(bf16[4,128,128]{2,1,0:T(8,128)(2,1)S(1)} %get-tuple-element.55), channel_id=1, source_target_pairs={{0,32},{8,40},{16,48},{24,56},{32,0},{40,8},{48,16},{56,24},{1,33}... | collective-permute-start | bytes 393224 | tf_op jit(solution)/shard_map/ppermute | solution.py:287
  136.0 2.5 %collective-permute-start.31 = (bf16[4,128,128]{2,1,0:T(8,128)(2,1)S(1)}, bf16[4,128,128]{2,1,0:T(8,128)(2,1)S(1)}, u32[]{:S(2)}, u32[]{:S(2)}) collective-permute-start(bf16[4,128,128]{2,1,0:T(8,128)(2,1)S(1)} %get-tuple-element.56), channel_id=1, source_target_pairs={{0,40},{8,48},{16,56},{24,0},{32,8},{40,16},{48,24},{56,32},{1,41}... | collective-permute-start | bytes 393224 | tf_op jit(solution)/shard_map/ppermute | solution.py:287
  138.5 2.4 %collective-permute-start.32 = (bf16[4,128,128]{2,1,0:T(8,128)(2,1)S(1)}, bf16[4,128,128]{2,1,0:T(8,128)(2,1)S(1)}, u32[]{:S(2)}, u32[]{:S(2)}) collective-permute-start(bf16[4,128,128]{2,1,0:T(8,128)(2,1)S(1)} %get-tuple-element.57), channel_id=1, source_target_pairs={{0,48},{8,56},{16,0},{24,8},{32,16},{40,24},{48,32},{56,40},{1,49}... | collective-permute-start | bytes 393224 | tf_op jit(solution)/shard_map/ppermute | solution.py:287
  141.0 7.6 %collective-permute-done.29.refs_3_ = bf16[4,128,128]{2,1,0:T(8,128)(2,1)S(1)} collective-permute-done((bf16[4,128,128]{2,1,0:T(8,128)(2,1)S(1)}, bf16[4,128,128]{2,1,0:T(8,128)(2,1)S(1)}, u32[]{:S(2)}, u32[]{:S(2)}) %collective-permute-start.29) | collective-permute-done | bytes 131104 | tf_op jit(solution)/shard_map/ppermute | solution.py:287
  148.5 0.7 collective-permute-done.30.refs_4_
  149.3 2.1 %collective-permute-done.31.refs_5_ = bf16[4,128,128]{2,1,0:T(8,128)(2,1)S(1)} collective-permute-done((bf16[4,128,128]{2,1,0:T(8,128)(2,1)S(1)}, bf16[4,128,128]{2,1,0:T(8,128)(2,1)S(1)}, u32[]{:S(2)}, u32[]{:S(2)}) %collective-permute-start.31) | collective-permute-done | bytes 131104 | tf_op jit(solution)/shard_map/ppermute | solution.py:287
  151.3 7.2 %collective-permute-done.32.refs_6_ = bf16[4,128,128]{2,1,0:T(8,128)(2,1)S(1)} collective-permute-done((bf16[4,128,128]{2,1,0:T(8,128)(2,1)S(1)}, bf16[4,128,128]{2,1,0:T(8,128)(2,1)S(1)}, u32[]{:S(2)}, u32[]{:S(2)}) %collective-permute-start.32) | collective-permute-done | bytes 131104 | tf_op jit(solution)/shard_map/ppermute | solution.py:287
  158.5 0.6 collective-permute-done.33.refs_7_
  159.1 1.8 %join.1 = (bf16[179,1024]{1,0:T(8,128)(2,1)}, bf16[32,128,128]{2,1,0:T(8,128)(2,1)}) custom-call(bf16[179,128]{1,0:T(8,128)(2,1)S(1)} %get-tuple-element.50.a_ref, bf16[179,128]{1,0:T(8,128)(2,1)S(1)} %collective-permute-done.24.b_ref, bf16[2,179,128]{2,1,0:T(8,128)(2,1)S(1)} %collective-permute-done.25.c_ref, ...), custom_call_target="tpu_custom_call" | custom-call | tf_op jit(solution)/shard_map/join/pallas_call | solution.py:257
  (52 shorter events, 2.1 us)
Async XLA Ops:
  5.9 18.0 %collective-permute-start.13 = (bf16[8,384,128]{2,1,0:T(8,128)(2,1)S(1)}, bf16[8,384,128]{2,1,0:T(8,128)(2,1)S(1)}, u32[]{:S(2)}, u32[]{:S(2)}) collective-permute-start(bf16[8,384,128]{2,1,0:T(8,128)(2,1)S(1)} %mm.20), channel_id=1, source_target_pairs={{0,1},{1,0},{2,3},{3,2},{4,5},{5,4},{6,7},{7,6},{8,9},{9,8},{10,11... | collective-permute-start | bytes 2359304 | tf_op jit(solution)/shard_map/ppermute | solution.py:287
  10.1 18.4 %collective-permute-start.19 = (bf16[8,400,128]{2,1,0:T(8,128)(2,1)S(1)}, bf16[8,400,128]{2,1,0:T(8,128)(2,1)S(1)}, u32[]{:S(2)}, u32[]{:S(2)}) collective-permute-start(bf16[8,400,128]{2,1,0:T(8,128)(2,1)S(1)} %mm.23), channel_id=1, source_target_pairs={{0,1},{1,0},{2,3},{3,2},{4,5},{5,4},{6,7},{7,6},{8,9},{9,8},{10,11... | collective-permute-start | bytes 2457608 | tf_op jit(solution)/shard_map/ppermute | solution.py:287
  12.4 19.8 %collective-permute-start.12 = (bf16[8,384,128]{2,1,0:T(8,128)(2,1)S(1)}, bf16[8,384,128]{2,1,0:T(8,128)(2,1)S(1)}, u32[]{:S(2)}, u32[]{:S(2)}) collective-permute-start(bf16[8,384,128]{2,1,0:T(8,128)(2,1)S(1)} %get-tuple-element.42), channel_id=1, source_target_pairs={{0,1},{1,0},{2,3},{3,2},{4,5},{5,4},{6,7},{7,6},{8,9},{9,8},{10,11... | collective-permute-start | bytes 2359304 | tf_op jit(solution)/shard_map/ppermute | solution.py:287
  14.1 15.1 %collective-permute-start.7 = (bf16[8,512,128]{2,1,0:T(8,128)(2,1)S(1)}, bf16[8,512,128]{2,1,0:T(8,128)(2,1)S(1)}, u32[]{:S(2)}, u32[]{:S(2)}) collective-permute-start(bf16[8,512,128]{2,1,0:T(8,128)(2,1)S(1)} %mm.17), channel_id=1, source_target_pairs={{0,1},{1,0},{2,3},{3,2},{4,5},{5,4},{6,7},{7,6},{8,9},{9,8},{10,11... | collective-permute-start | bytes 3145736 | tf_op jit(solution)/shard_map/ppermute | solution.py:287
  15.3 29.4 %collective-permute-start.1 = (bf16[8,512,128]{2,1,0:T(8,128)(2,1)S(1)}, bf16[8,512,128]{2,1,0:T(8,128)(2,1)S(1)}, u32[]{:S(2)}, u32[]{:S(2)}) collective-permute-start(bf16[8,512,128]{2,1,0:T(8,128)(2,1)S(1)} %mm.14), channel_id=1, source_target_pairs={{0,1},{1,0},{2,3},{3,2},{4,5},{5,4},{6,7},{7,6},{8,9},{9,8},{10,11... | collective-permute-start | bytes 3145736 | tf_op jit(solution)/shard_map/ppermute | solution.py:287
  24.2 20.4 %collective-permute-start.14 = (bf16[8,384,128]{2,1,0:T(8,128)(2,1)S(1)}, bf16[8,384,128]{2,1,0:T(8,128)(2,1)S(1)}, u32[]{:S(2)}, u32[]{:S(2)}) collective-permute-start(bf16[8,384,128]{2,1,0:T(8,128)(2,1)S(1)} %add_convert_fusion.3), channel_id=1, source_target_pairs={{2,4},{4,2},{6,0},{0,6},{3,5},{5,3},{7,1},{1,7},{10,12},{12,10},{1... | collective-permute-start | bytes 2359304 | tf_op jit(solution)/shard_map/ppermute | solution.py:287
  28.5 18.0 %collective-permute-start.18 = (bf16[8,400,128]{2,1,0:T(8,128)(2,1)S(1)}, bf16[8,400,128]{2,1,0:T(8,128)(2,1)S(1)}, u32[]{:S(2)}, u32[]{:S(2)}) collective-permute-start(bf16[8,400,128]{2,1,0:T(8,128)(2,1)S(1)} %get-tuple-element.45), channel_id=1, source_target_pairs={{0,1},{1,0},{2,3},{3,2},{4,5},{5,4},{6,7},{7,6},{8,9},{9,8},{10,11... | collective-permute-start | bytes 2457608 | tf_op jit(solution)/shard_map/ppermute | solution.py:287
  29.1 21.0 %collective-permute-start.20 = (bf16[8,400,128]{2,1,0:T(8,128)(2,1)S(1)}, bf16[8,400,128]{2,1,0:T(8,128)(2,1)S(1)}, u32[]{:S(2)}, u32[]{:S(2)}) collective-permute-start(bf16[8,400,128]{2,1,0:T(8,128)(2,1)S(1)} %add_convert_fusion.2), channel_id=1, source_target_pairs={{64,128},{128,64},{192,0},{0,192},{65,129},{129,65},{193,1},{1,193... | collective-permute-start | bytes 2457608 | tf_op jit(solution)/shard_map/ppermute | solution.py:287
  32.3 49.9 %collective-permute-start.6 = (bf16[8,512,128]{2,1,0:T(8,128)(2,1)S(1)}, bf16[8,512,128]{2,1,0:T(8,128)(2,1)S(1)}, u32[]{:S(2)}, u32[]{:S(2)}) collective-permute-start(bf16[8,512,128]{2,1,0:T(8,128)(2,1)S(1)} %get-tuple-element.39), channel_id=1, source_target_pairs={{0,1},{1,0},{2,3},{3,2},{4,5},{5,4},{6,7},{7,6},{8,9},{9,8},{10,11... | collective-permute-start | bytes 3145736 | tf_op jit(solution)/shard_map/ppermute | solution.py:287
  44.5 37.7 %collective-permute-start.8 = (bf16[8,512,128]{2,1,0:T(8,128)(2,1)S(1)}, bf16[8,512,128]{2,1,0:T(8,128)(2,1)S(1)}, u32[]{:S(2)}, u32[]{:S(2)}) collective-permute-start(bf16[8,512,128]{2,1,0:T(8,128)(2,1)S(1)} %add_convert_fusion), channel_id=1, source_target_pairs={{0,64},{64,0},{128,192},{192,128},{1,65},{65,1},{129,193},{193,129... | collective-permute-start | bytes 3145736 | tf_op jit(solution)/shard_map/ppermute | solution.py:287
  44.7 13.9 %collective-permute-start.15 = (bf16[4,384,128]{2,1,0:T(8,128)(2,1)S(1)}, bf16[4,384,128]{2,1,0:T(8,128)(2,1)S(1)}, u32[]{:S(2)}, u32[]{:S(2)}) collective-permute-start(bf16[4,384,128]{2,1,0:T(8,128)(2,1)S(1)} %add_convert_fusion.7), channel_id=1, source_target_pairs={{64,128},{128,64},{192,0},{0,192},{65,129},{129,65},{193,1},{1,193... | collective-permute-start | bytes 1179656 | tf_op jit(solution)/shard_map/ppermute | solution.py:287
  46.6 38.0 %collective-permute-start = (bf16[8,512,128]{2,1,0:T(8,128)(2,1)S(1)}, bf16[8,512,128]{2,1,0:T(8,128)(2,1)S(1)}, u32[]{:S(2)}, u32[]{:S(2)}) collective-permute-start(bf16[8,512,128]{2,1,0:T(8,128)(2,1)S(1)} %get-tuple-element.36), channel_id=1, source_target_pairs={{0,1},{1,0},{2,3},{3,2},{4,5},{5,4},{6,7},{7,6},{8,9},{9,8},{10,11... | collective-permute-start | bytes 3145736 | tf_op jit(solution)/shard_map/ppermute | solution.py:287
  50.2 34.4 %collective-permute-start.2 = (bf16[8,512,128]{2,1,0:T(8,128)(2,1)S(1)}, bf16[8,512,128]{2,1,0:T(8,128)(2,1)S(1)}, u32[]{:S(2)}, u32[]{:S(2)}) collective-permute-start(bf16[8,512,128]{2,1,0:T(8,128)(2,1)S(1)} %add_convert_fusion.1), channel_id=1, source_target_pairs={{0,2},{2,0},{4,6},{6,4},{1,3},{3,1},{5,7},{7,5},{8,10},{10,8},{12,... | collective-permute-start | bytes 3145736 | tf_op jit(solution)/shard_map/ppermute | solution.py:287
  58.6 23.4 %collective-permute-start.21 = (bf16[4,400,128]{2,1,0:T(8,128)(2,1)S(1)}, bf16[4,400,128]{2,1,0:T(8,128)(2,1)S(1)}, u32[]{:S(2)}, u32[]{:S(2)}) collective-permute-start(bf16[4,400,128]{2,1,0:T(8,128)(2,1)S(1)} %add_convert_fusion.6), channel_id=1, source_target_pairs={{0,2},{2,0},{4,6},{6,4},{1,3},{3,1},{5,7},{7,5},{8,10},{10,8},{12,... | collective-permute-start | bytes 1228808 | tf_op jit(solution)/shard_map/ppermute | solution.py:287
  82.0 4.5 %collective-permute-start.16 = (bf16[2,384,128]{2,1,0:T(8,128)(2,1)S(1)}, bf16[2,384,128]{2,1,0:T(8,128)(2,1)S(1)}, u32[]{:S(2)}, u32[]{:S(2)}) collective-permute-start(bf16[2,384,128]{2,1,0:T(8,128)(2,1)S(1)} %add_convert_fusion.11), channel_id=1, source_target_pairs={{0,2},{2,0},{4,6},{6,4},{1,3},{3,1},{5,7},{7,5},{8,10},{10,8},{12,... | collective-permute-start | bytes 589832 | tf_op jit(solution)/shard_map/ppermute | solution.py:287
  82.2 4.7 %collective-permute-start.22 = (bf16[2,400,128]{2,1,0:T(8,128)(2,1)S(1)}, bf16[2,400,128]{2,1,0:T(8,128)(2,1)S(1)}, u32[]{:S(2)}, u32[]{:S(2)}) collective-permute-start(bf16[2,400,128]{2,1,0:T(8,128)(2,1)S(1)} %add_convert_fusion.10), channel_id=1, source_target_pairs={{0,64},{64,0},{128,192},{192,128},{1,65},{65,1},{129,193},{193,129... | collective-permute-start | bytes 614408 | tf_op jit(solution)/shard_map/ppermute | solution.py:287
  82.5 18.0 %collective-permute-start.9 = (bf16[4,512,128]{2,1,0:T(8,128)(2,1)S(1)}, bf16[4,512,128]{2,1,0:T(8,128)(2,1)S(1)}, u32[]{:S(2)}, u32[]{:S(2)}) collective-permute-start(bf16[4,512,128]{2,1,0:T(8,128)(2,1)S(1)} %add_convert_fusion.4), channel_id=1, source_target_pairs={{2,4},{4,2},{6,0},{0,6},{3,5},{5,3},{7,1},{1,7},{10,12},{12,10},{1... | collective-permute-start | bytes 1572872 | tf_op jit(solution)/shard_map/ppermute | solution.py:287
  84.8 17.3 %collective-permute-start.3 = (bf16[4,512,128]{2,1,0:T(8,128)(2,1)S(1)}, bf16[4,512,128]{2,1,0:T(8,128)(2,1)S(1)}, u32[]{:S(2)}, u32[]{:S(2)}) collective-permute-start(bf16[4,512,128]{2,1,0:T(8,128)(2,1)S(1)} %add_convert_fusion.5), channel_id=1, source_target_pairs={{0,64},{64,0},{128,192},{192,128},{1,65},{65,1},{129,193},{193,129... | collective-permute-start | bytes 1572872 | tf_op jit(solution)/shard_map/ppermute | solution.py:287
  86.6 13.8 %collective-permute-start.17 = (bf16[1,384,128]{2,1,0:T(8,128)(2,1)S(1)}, bf16[1,384,128]{2,1,0:T(8,128)(2,1)S(1)}, u32[]{:S(2)}, u32[]{:S(2)}) collective-permute-start(bf16[1,384,128]{2,1,0:T(8,128)(2,1)S(1)} %add_convert_fusion.15), channel_id=1, source_target_pairs={{0,64},{64,0},{128,192},{192,128},{1,65},{65,1},{129,193},{193,129... | collective-permute-start | bytes 294920 | tf_op jit(solution)/shard_map/ppermute | solution.py:287
  86.9 16.9 %collective-permute-start.23 = (bf16[1,400,128]{2,1,0:T(8,128)(2,1)S(1)}, bf16[1,400,128]{2,1,0:T(8,128)(2,1)S(1)}, u32[]{:S(2)}, u32[]{:S(2)}) collective-permute-start(bf16[1,400,128]{2,1,0:T(8,128)(2,1)S(1)} %add_convert_fusion.14), channel_id=1, source_target_pairs={{2,4},{4,2},{6,0},{0,6},{3,5},{5,3},{7,1},{1,7},{10,12},{12,10},{1... | collective-permute-start | bytes 307208 | tf_op jit(solution)/shard_map/ppermute | solution.py:287
  100.6 6.5 %collective-permute-start.10 = (bf16[2,512,128]{2,1,0:T(8,128)(2,1)S(1)}, bf16[2,512,128]{2,1,0:T(8,128)(2,1)S(1)}, u32[]{:S(2)}, u32[]{:S(2)}) collective-permute-start(bf16[2,512,128]{2,1,0:T(8,128)(2,1)S(1)} %add_convert_fusion.8), channel_id=1, source_target_pairs={{64,128},{128,64},{192,0},{0,192},{65,129},{129,65},{193,1},{1,193... | collective-permute-start | bytes 786440 | tf_op jit(solution)/shard_map/ppermute | solution.py:287
  102.3 12.2 %copy-start.3 = (s32[1,179]{1,0:T(1,128)S(1)}, s32[1,179]{1,0:T(1,128)}, u32[]{:S(2)}) copy-start(s32[1,179]{1,0:T(1,128)} %ids_ref.1) | copy-start | bytes 2152
  102.3 12.1 %copy-start.4 = (s32[14,1]{0,1:T(1,128)S(1)}, s32[14,1]{0,1:T(1,128)}, u32[]{:S(2)}) copy-start(s32[14,1]{0,1:T(1,128)} %param.12) | copy-start | bytes 172
  102.3 6.8 %collective-permute-start.4 = (bf16[2,512,128]{2,1,0:T(8,128)(2,1)S(1)}, bf16[2,512,128]{2,1,0:T(8,128)(2,1)S(1)}, u32[]{:S(2)}, u32[]{:S(2)}) collective-permute-start(bf16[2,512,128]{2,1,0:T(8,128)(2,1)S(1)} %add_convert_fusion.9), channel_id=1, source_target_pairs={{2,4},{4,2},{6,0},{0,6},{3,5},{5,3},{7,1},{1,7},{10,12},{12,10},{1... | collective-permute-start | bytes 786440 | tf_op jit(solution)/shard_map/ppermute | solution.py:287
  107.2 8.9 %copy-start = (f32[179,128]{1,0:T(8,128)S(1)}, f32[179,128]{1,0:T(8,128)}, u32[]{:S(2)}) copy-start(f32[179,128]{1,0:T(8,128)} %ma_ref.1) | copy-start | bytes 274948
  107.2 8.9 %copy-start.1 = (f32[179,128]{1,0:T(8,128)S(1)}, f32[179,128]{1,0:T(8,128)}, u32[]{:S(2)}) copy-start(f32[179,128]{1,0:T(8,128)} %mo_ref.1) | copy-start | bytes 274948
  107.2 8.9 %copy-start.2 = (f32[179,128]{1,0:T(8,128)S(1)}, f32[179,128]{1,0:T(8,128)}, u32[]{:S(2)}) copy-start(f32[179,128]{1,0:T(8,128)} %se_ref.1) | copy-start | bytes 274948
  107.3 4.2 %collective-permute-start.11 = (bf16[1,512,128]{2,1,0:T(8,128)(2,1)S(1)}, bf16[1,512,128]{2,1,0:T(8,128)(2,1)S(1)}, u32[]{:S(2)}, u32[]{:S(2)}) collective-permute-start(bf16[1,512,128]{2,1,0:T(8,128)(2,1)S(1)} %add_convert_fusion.12), channel_id=1, source_target_pairs={{0,2},{2,0},{4,6},{6,4},{1,3},{3,1},{5,7},{7,5},{8,10},{10,8},{12,... | collective-permute-start | bytes 393224 | tf_op jit(solution)/shard_map/ppermute | solution.py:287
  109.2 5.1 %collective-permute-start.5 = (bf16[1,512,128]{2,1,0:T(8,128)(2,1)S(1)}, bf16[1,512,128]{2,1,0:T(8,128)(2,1)S(1)}, u32[]{:S(2)}, u32[]{:S(2)}) collective-permute-start(bf16[1,512,128]{2,1,0:T(8,128)(2,1)S(1)} %add_convert_fusion.13), channel_id=1, source_target_pairs={{64,128},{128,64},{192,0},{0,192},{65,129},{129,65},{193,1},{1,193... | collective-permute-start | bytes 393224 | tf_op jit(solution)/shard_map/ppermute | solution.py:287
  116.9 6.9 %collective-permute-start.24 = (bf16[179,128]{1,0:T(8,128)(2,1)S(1)}, bf16[179,128]{1,0:T(8,128)(2,1)S(1)}, u32[]{:S(2)}, u32[]{:S(2)}) collective-permute-start(bf16[179,128]{1,0:T(8,128)(2,1)S(1)} %get-tuple-element.50.a_ref), channel_id=1, source_target_pairs={{0,1},{1,0},{2,3},{3,2},{4,5},{5,4},{6,7},{7,6},{8,9},{9,8},{10,11... | collective-permute-start | bytes 137480 | tf_op jit(solution)/shard_map/ppermute | solution.py:287
  123.8 8.7 %collective-permute-start.25 = (bf16[2,179,128]{2,1,0:T(8,128)(2,1)S(1)}, bf16[2,179,128]{2,1,0:T(8,128)(2,1)S(1)}, u32[]{:S(2)}, u32[]{:S(2)}) collective-permute-start(bf16[2,179,128]{2,1,0:T(8,128)(2,1)S(1)} %pad_maximum_fusion.1), channel_id=1, source_target_pairs={{0,2},{2,0},{4,6},{6,4},{1,3},{3,1},{5,7},{7,5},{8,10},{10,8},{12,... | collective-permute-start | bytes 274952 | tf_op jit(solution)/shard_map/ppermute | solution.py:287
  124.2 11.8 %collective-permute-start.27 = (bf16[4,128,128]{2,1,0:T(8,128)(2,1)S(1)}, bf16[4,128,128]{2,1,0:T(8,128)(2,1)S(1)}, u32[]{:S(2)}, u32[]{:S(2)}) collective-permute-start(bf16[4,128,128]{2,1,0:T(8,128)(2,1)S(1)} %get-tuple-element.52), channel_id=1, source_target_pairs={{0,8},{8,16},{16,24},{24,32},{32,40},{40,48},{48,56},{56,0},{1,9},... | collective-permute-start | bytes 393224 | tf_op jit(solution)/shard_map/ppermute | solution.py:287
  125.8 12.8 %collective-permute-start.28 = (bf16[4,128,128]{2,1,0:T(8,128)(2,1)S(1)}, bf16[4,128,128]{2,1,0:T(8,128)(2,1)S(1)}, u32[]{:S(2)}, u32[]{:S(2)}) collective-permute-start(bf16[4,128,128]{2,1,0:T(8,128)(2,1)S(1)} %get-tuple-element.53), channel_id=1, source_target_pairs={{0,16},{8,24},{16,32},{24,40},{32,48},{40,56},{48,0},{56,8},{1,17}... | collective-permute-start | bytes 393224 | tf_op jit(solution)/shard_map/ppermute | solution.py:287
  128.8 19.8 %collective-permute-start.29 = (bf16[4,128,128]{2,1,0:T(8,128)(2,1)S(1)}, bf16[4,128,128]{2,1,0:T(8,128)(2,1)S(1)}, u32[]{:S(2)}, u32[]{:S(2)}) collective-permute-start(bf16[4,128,128]{2,1,0:T(8,128)(2,1)S(1)} %get-tuple-element.54), channel_id=1, source_target_pairs={{0,24},{8,32},{16,40},{24,48},{32,56},{40,0},{48,8},{56,16},{1,25}... | collective-permute-start | bytes 393224 | tf_op jit(solution)/shard_map/ppermute | solution.py:287
  132.5 26.6 %collective-permute-start.26 = (bf16[4,179,128]{2,1,0:T(8,128)(2,1)S(1)}, bf16[4,179,128]{2,1,0:T(8,128)(2,1)S(1)}, u32[]{:S(2)}, u32[]{:S(2)}) collective-permute-start(bf16[4,179,128]{2,1,0:T(8,128)(2,1)S(1)} %pad_maximum_fusion), channel_id=1, source_target_pairs={{2,4},{4,2},{6,0},{0,6},{3,5},{5,3},{7,1},{1,7},{10,12},{12,10},{1... | collective-permute-start | bytes 549896 | tf_op jit(solution)/shard_map/ppermute | solution.py:287
  133.6 15.7 %collective-permute-start.30 = (bf16[4,128,128]{2,1,0:T(8,128)(2,1)S(1)}, bf16[4,128,128]{2,1,0:T(8,128)(2,1)S(1)}, u32[]{:S(2)}, u32[]{:S(2)}) collective-permute-start(bf16[4,128,128]{2,1,0:T(8,128)(2,1)S(1)} %get-tuple-element.55), channel_id=1, source_target_pairs={{0,32},{8,40},{16,48},{24,56},{32,0},{40,8},{48,16},{56,24},{1,33}... | collective-permute-start | bytes 393224 | tf_op jit(solution)/shard_map/ppermute | solution.py:287
  136.0 15.3 %collective-permute-start.31 = (bf16[4,128,128]{2,1,0:T(8,128)(2,1)S(1)}, bf16[4,128,128]{2,1,0:T(8,128)(2,1)S(1)}, u32[]{:S(2)}, u32[]{:S(2)}) collective-permute-start(bf16[4,128,128]{2,1,0:T(8,128)(2,1)S(1)} %get-tuple-element.56), channel_id=1, source_target_pairs={{0,40},{8,48},{16,56},{24,0},{32,8},{40,16},{48,24},{56,32},{1,41}... | collective-permute-start | bytes 393224 | tf_op jit(solution)/shard_map/ppermute | solution.py:287
  138.5 20.0 %collective-permute-start.32 = (bf16[4,128,128]{2,1,0:T(8,128)(2,1)S(1)}, bf16[4,128,128]{2,1,0:T(8,128)(2,1)S(1)}, u32[]{:S(2)}, u32[]{:S(2)}) collective-permute-start(bf16[4,128,128]{2,1,0:T(8,128)(2,1)S(1)} %get-tuple-element.57), channel_id=1, source_target_pairs={{0,48},{8,56},{16,0},{24,8},{32,16},{40,24},{48,32},{56,40},{1,49}... | collective-permute-start | bytes 393224 | tf_op jit(solution)/shard_map/ppermute | solution.py:287
  148.5 10.6 %collective-permute-start.33 = (bf16[4,128,128]{2,1,0:T(8,128)(2,1)S(1)}, bf16[4,128,128]{2,1,0:T(8,128)(2,1)S(1)}, u32[]{:S(2)}, u32[]{:S(2)}) collective-permute-start(bf16[4,128,128]{2,1,0:T(8,128)(2,1)S(1)} %get-tuple-element.58), channel_id=1, source_target_pairs={{0,56},{8,0},{16,8},{24,16},{32,24},{40,32},{48,40},{56,48},{1,57}... | collective-permute-start | bytes 393224 | tf_op jit(solution)/shard_map/ppermute | solution.py:287
where the time goes:
time: 162 us; the launch traced here: 161 us
  waiting for transfers between devices  84.2 us (52%)
  starting transfers between devices  46.7 us (29%)
  Pallas kernels  25.4 us (16%)
  other arithmetic  2.91 us (2%)
  between operations  1.84 us (1%)
    ppermute x34, waiting for transfers between devices, moved(): return lax.ppermute(v, axis, pairs)  84.2 us
    ppermute x34, starting transfers between devices, moved(): return lax.ppermute(v, axis, pairs)  46.7 us
    pallas_call x12, Pallas kernels, product(): pl.pallas_call(functools.partial(mm_kernel, spare=spare, k=k, half=half,...  17.5 us
    pallas_call x1, Pallas kernels, loaded(): pl.pallas_call(load_kernel, grid_spec=pltpu.PrefetchScalarGridSpec(num_sc...  3.71 us
  transfers between devices with their start and end apart: 34, of which 17 were waited for; matrix products, arithmetic and copies ran while one was open for 2% of the time, Pallas kernels for 10%

commit v1 on v0

--- a/solution.py
+++ b/solution.py
@@ -18,7 +18,7 @@
 ODD = [(1, 2), (2, 1), (3, 0), (0, 3)]
 DIMS = (("pipe_0", EVEN), ("dp", EVEN), ("pipe_0", ODD), ("dp", ODD))
 SWAP = [(0, 1), (1, 0)]
-ORDERS = ((0, 1, 2, 3), (1, 2, 3, 0), (2, 3, 0, 1), (3, 0, 1, 2))
+ORDERS = ((0, 1, 3, 2), (1, 0, 2, 3), (2, 3, 0, 1), (3, 2, 1, 0))
 MiB = 1 << 20
 
 
@@ -160,18 +160,18 @@
     for (first, nblk), g in zip(COLOURS, (g0, g1, g2, g3)):
         acc[first * CB : (first + nblk) * CB, :] = g[: nblk * CB, :]
     digits = g3[COLOURS[3][1] * CB : COLOURS[3][1] * CB + 8, :]
-    total = digits[0:1, :] + 8.0 * digits[1:2, :] + 64.0 * digits[2:3, :]
+    scale = 1.0 / (digits[0:1, :] + 8.0 * digits[1:2, :] + 64.0 * digits[2:3, :])
     pack[...] = jnp.zeros_like(pack)
 
     def take(i, _):
         h = ids_ref[0, i]
-        hot_ref[pl.ds(i, 1), :] = acc[pl.ds(h, 1), :] / total
+        hot_ref[pl.ds(i, 1), :] = acc[pl.ds(h, 1), :] * scale
         acc[pl.ds(h, 1), :] = jnp.zeros((1, CB), jnp.float32)
         return 0
 
     lax.fori_loop(0, hot_ref.shape[0], take, 0, unroll=4)
     for b in range(acc.shape[0] // CB):
-        x = acc[b * CB : (b + 1) * CB, :] / total
+        x = acc[b * CB : (b + 1) * CB, :] * scale
         owner = own_ref[b]
         slot = jnp.int32(0)
         for e in range(b):

time: 162 us -> 152 us (0.938)
  waiting for transfers between devices: 84.2 us -> 74.9 us
    ppermute x34, waiting for transfers between devices: 84.2 us -> 74.9 us  [moved(): return lax.ppermute(v, axis, pairs)]
  transfers between devices with their start and end apart: 34 -> 34, of which waited for: 17 -> 17; matrix products, arithmetic and copies ran while one was open for 2% -> 2% of each run, Pallas kernels for 10% -> 11%
where the time goes in v1:
time: 152 us; the launch traced here: 151 us
  waiting for transfers between devices  74.9 us (49%)
  starting transfers between devices  45.9 us (30%)
  Pallas kernels  25.3 us (17%)
  other arithmetic  2.91 us (2%)
  between operations  1.85 us (1%)
    ppermute x34, waiting for transfers between devices, moved(): return lax.ppermute(v, axis, pairs)  74.9 us
    ppermute x34, starting transfers between devices, moved(): return lax.ppermute(v, axis, pairs)  45.9 us
    pallas_call x12, Pallas kernels, product(): pl.pallas_call(functools.partial(mm_kernel, spare=spare, k=k, half=half,...  17.5 us
    pallas_call x1, Pallas kernels, loaded(): pl.pallas_call(load_kernel, grid_spec=pltpu.PrefetchScalarGridSpec(num_sc...  3.71 us
  transfers between devices with their start and end apart: 34, of which 17 were waited for; matrix products, arithmetic and copies ran while one was open for 2% of the time, Pallas kernels for 11%

profile of v1, /device:TPU:1, one launch (start us, length us, event | category | flops | bytes accessed | tf_op | source)
XLA Modules:
  0.0 150.9 jit_solution(10064678216077104310)
XLA Ops:
  1.3 3.7 %load.1 = (bf16[768,4096]{1,0:T(8,128)(2,1)S(1)}, bf16[512,768]{1,0:T(8,128)(2,1)S(1)}, bf16[512,768]{1,0:T(8,128)(2,1)S(1)}, bf16[384,768]{1,0:T(8,128)(2,1)S(1)}, bf16[384,768]{1,0:T(8,128)(2,1)S(1)}) custom-call(s32[1]{0:T(128)S(6)} %copy.13.cnt_ref, bf16[768,4096]{1,0:T(8,128)(2,1)} %a_hbm.1, bf16[768,1792]{1,0:T(8,128)(2,1)} %g_hbm.1), custom_call_target="tpu_custom_call" | custom-call | flops 2000000000 | tf_op jit(solution)/shard_map/load/pallas_call | solution.py:81
  5.0 0.9 mm.20
  5.9 3.3 %collective-permute-start.13 = (bf16[8,384,128]{2,1,0:T(8,128)(2,1)S(1)}, bf16[8,384,128]{2,1,0:T(8,128)(2,1)S(1)}, u32[]{:S(2)}, u32[]{:S(2)}) collective-permute-start(bf16[8,384,128]{2,1,0:T(8,128)(2,1)S(1)} %mm.20), channel_id=1, source_target_pairs={{0,1},{1,0},{2,3},{3,2},{4,5},{5,4},{6,7},{7,6},{8,9},{9,8},{10,11... | collective-permute-start | bytes 2359304 | tf_op jit(solution)/shard_map/ppermute | solution.py:287
  9.2 0.9 mm.23
  10.2 2.2 %mm.18 = (bf16[8,384,128]{2,1,0:T(8,128)(2,1)S(1)}, bf16[8,384,128]{2,1,0:T(8,128)(2,1)S(1)}) custom-call(s32[1]{0:T(128)S(6)} %copy.13.cnt_ref, bf16[384,768]{1,0:T(8,128)(2,1)S(1)} %get-tuple-element.40.l_ref, bf16[768,4096]{1,0:T(8,128)(2,1)S(1)} %get-tuple-element.34.a_ref), custom_call_target="tpu_custom_call" | custom-call | flops 1207959552 | tf_op jit(solution)/shard_map/mm/pallas_call | solution.py:138
  12.4 0.6 collective-permute-start.12
  13.0 1.0 mm.17
  14.2 1.1 mm.14
  15.3 0.7 collective-permute-start.1
  16.0 1.1 mm.16
  17.1 1.1 mm.13
  18.2 0.9 mm.19
  19.1 2.2 %mm.21 = (bf16[8,400,128]{2,1,0:T(8,128)(2,1)S(1)}, bf16[8,400,128]{2,1,0:T(8,128)(2,1)S(1)}) custom-call(s32[1]{0:T(128)S(6)} %copy.13.cnt_ref, bf16[384,768]{1,0:T(8,128)(2,1)S(1)} %get-tuple-element.43.l_ref, bf16[768,4096]{1,0:T(8,128)(2,1)S(1)} %get-tuple-element.34.a_ref), custom_call_target="tpu_custom_call" | custom-call | flops 1207959552 | tf_op jit(solution)/shard_map/mm/pallas_call | solution.py:138
  21.3 2.6 %mm.15 = (bf16[8,512,128]{2,1,0:T(8,128)(2,1)S(1)}, bf16[8,512,128]{2,1,0:T(8,128)(2,1)S(1)}) custom-call(s32[1]{0:T(128)S(6)} %copy.13.cnt_ref, bf16[512,768]{1,0:T(8,128)(2,1)S(1)} %get-tuple-element.37.l_ref, bf16[768,4096]{1,0:T(8,128)(2,1)S(1)} %get-tuple-element.34.a_ref), custom_call_target="tpu_custom_call" | custom-call | flops 1610612736 | tf_op jit(solution)/shard_map/mm/pallas_call | solution.py:138
  23.9 0.2 add_convert_fusion.3
  24.1 0.9 collective-permute-start.14
  25.0 0.9 mm.22
  25.9 2.6 %mm.12 = (bf16[8,512,128]{2,1,0:T(8,128)(2,1)S(1)}, bf16[8,512,128]{2,1,0:T(8,128)(2,1)S(1)}) custom-call(s32[1]{0:T(128)S(6)} %copy.13.cnt_ref, bf16[512,768]{1,0:T(8,128)(2,1)S(1)} %get-tuple-element.33.l_ref, bf16[768,4096]{1,0:T(8,128)(2,1)S(1)} %get-tuple-element.34.a_ref), custom_call_target="tpu_custom_call" | custom-call | flops 1610612736 | tf_op jit(solution)/shard_map/mm/pallas_call | solution.py:138
  28.5 0.4 collective-permute-start.18
  28.9 0.2 add_convert_fusion.2
  29.1 2.8 %collective-permute-start.20 = (bf16[8,400,128]{2,1,0:T(8,128)(2,1)S(1)}, bf16[8,400,128]{2,1,0:T(8,128)(2,1)S(1)}, u32[]{:S(2)}, u32[]{:S(2)}) collective-permute-start(bf16[8,400,128]{2,1,0:T(8,128)(2,1)S(1)} %add_convert_fusion.2), channel_id=1, source_target_pairs={{64,128},{128,64},{192,0},{0,192},{65,129},{129,65},{193,1},{1,193... | collective-permute-start | bytes 2457608 | tf_op jit(solution)/shard_map/ppermute | solution.py:287
  31.9 0.3 add_convert_fusion
  32.2 0.6 collective-permute-start.6
  32.8 11.7 %collective-permute-done.14 = bf16[8,384,128]{2,1,0:T(8,128)(2,1)S(1)} collective-permute-done((bf16[8,384,128]{2,1,0:T(8,128)(2,1)S(1)}, bf16[8,384,128]{2,1,0:T(8,128)(2,1)S(1)}, u32[]{:S(2)}, u32[]{:S(2)}) %collective-permute-start.14) | collective-permute-done | bytes 786464 | tf_op jit(solution)/shard_map/ppermute | solution.py:287
  44.5 0.2 add_convert_fusion.7
  44.7 1.6 %collective-permute-start.15 = (bf16[4,384,128]{2,1,0:T(8,128)(2,1)S(1)}, bf16[4,384,128]{2,1,0:T(8,128)(2,1)S(1)}, u32[]{:S(2)}, u32[]{:S(2)}) collective-permute-start(bf16[4,384,128]{2,1,0:T(8,128)(2,1)S(1)} %add_convert_fusion.7), channel_id=1, source_target_pairs={{64,128},{128,64},{192,0},{0,192},{65,129},{129,65},{193,1},{1,193... | collective-permute-start | bytes 1179656 | tf_op jit(solution)/shard_map/ppermute | solution.py:287
  46.3 0.3 add_convert_fusion.1
  46.5 1.5 %collective-permute-start = (bf16[8,512,128]{2,1,0:T(8,128)(2,1)S(1)}, bf16[8,512,128]{2,1,0:T(8,128)(2,1)S(1)}, u32[]{:S(2)}, u32[]{:S(2)}) collective-permute-start(bf16[8,512,128]{2,1,0:T(8,128)(2,1)S(1)} %get-tuple-element.36), channel_id=1, source_target_pairs={{0,1},{1,0},{2,3},{3,2},{4,5},{5,4},{6,7},{7,6},{8,9},{9,8},{10,11... | collective-permute-start | bytes 3145736 | tf_op jit(solution)/shard_map/ppermute | solution.py:287
  48.1 2.0 %collective-permute-done.20 = bf16[8,400,128]{2,1,0:T(8,128)(2,1)S(1)} collective-permute-done((bf16[8,400,128]{2,1,0:T(8,128)(2,1)S(1)}, bf16[8,400,128]{2,1,0:T(8,128)(2,1)S(1)}, u32[]{:S(2)}, u32[]{:S(2)}) %collective-permute-start.20) | collective-permute-done | bytes 819232 | tf_op jit(solution)/shard_map/ppermute | solution.py:287
  50.1 0.2 add_convert_fusion.6
  50.3 8.3 %collective-permute-done.15 = bf16[4,384,128]{2,1,0:T(8,128)(2,1)S(1)} collective-permute-done((bf16[4,384,128]{2,1,0:T(8,128)(2,1)S(1)}, bf16[4,384,128]{2,1,0:T(8,128)(2,1)S(1)}, u32[]{:S(2)}, u32[]{:S(2)}) %collective-permute-start.15) | collective-permute-done | bytes 393248 | tf_op jit(solution)/shard_map/ppermute | solution.py:287
  58.5 1.8 %collective-permute-start.21 = (bf16[4,400,128]{2,1,0:T(8,128)(2,1)S(1)}, bf16[4,400,128]{2,1,0:T(8,128)(2,1)S(1)}, u32[]{:S(2)}, u32[]{:S(2)}) collective-permute-start(bf16[4,400,128]{2,1,0:T(8,128)(2,1)S(1)} %add_convert_fusion.6), channel_id=1, source_target_pairs={{2,4},{4,2},{6,0},{0,6},{3,5},{5,3},{7,1},{1,7},{10,12},{12,10},{1... | collective-permute-start | bytes 1228808 | tf_op jit(solution)/shard_map/ppermute | solution.py:287
  60.4 9.3 %collective-permute-done.21 = bf16[4,400,128]{2,1,0:T(8,128)(2,1)S(1)} collective-permute-done((bf16[4,400,128]{2,1,0:T(8,128)(2,1)S(1)}, bf16[4,400,128]{2,1,0:T(8,128)(2,1)S(1)}, u32[]{:S(2)}, u32[]{:S(2)}) %collective-permute-start.21) | collective-permute-done | bytes 409632 | tf_op jit(solution)/shard_map/ppermute | solution.py:287
  70.0 0.2 add_convert_fusion.4
  70.2 1.5 %collective-permute-start.9 = (bf16[4,512,128]{2,1,0:T(8,128)(2,1)S(1)}, bf16[4,512,128]{2,1,0:T(8,128)(2,1)S(1)}, u32[]{:S(2)}, u32[]{:S(2)}) collective-permute-start(bf16[4,512,128]{2,1,0:T(8,128)(2,1)S(1)} %add_convert_fusion.4), channel_id=1, source_target_pairs={{0,2},{2,0},{4,6},{6,4},{1,3},{3,1},{5,7},{7,5},{8,10},{10,8},{12,... | collective-permute-start | bytes 1572872 | tf_op jit(solution)/shard_map/ppermute | solution.py:287
  71.7 1.4 collective-permute-done.2
  73.1 0.2 add_convert_fusion.5
  73.5 3.9 %collective-permute-done.16 = bf16[2,384,128]{2,1,0:T(8,128)(2,1)S(1)} collective-permute-done((bf16[2,384,128]{2,1,0:T(8,128)(2,1)S(1)}, bf16[2,384,128]{2,1,0:T(8,128)(2,1)S(1)}, u32[]{:S(2)}, u32[]{:S(2)}) %collective-permute-start.16) | collective-permute-done | bytes 196640 | tf_op jit(solution)/shard_map/ppermute | solution.py:287
  77.8 8.7 %collective-permute-done.17 = bf16[1,384,128]{2,1,0:T(8,128)(2,1)S(1)} collective-permute-done((bf16[1,384,128]{2,1,0:T(8,128)(2,1)S(1)}, bf16[1,384,128]{2,1,0:T(8,128)(2,1)S(1)}, u32[]{:S(2)}, u32[]{:S(2)}) %collective-permute-start.17) | collective-permute-done | bytes 98336 | tf_op jit(solution)/shard_map/ppermute | solution.py:287
  86.5 2.1 %collective-permute-done.9 = bf16[4,512,128]{2,1,0:T(8,128)(2,1)S(1)} collective-permute-done((bf16[4,512,128]{2,1,0:T(8,128)(2,1)S(1)}, bf16[4,512,128]{2,1,0:T(8,128)(2,1)S(1)}, u32[]{:S(2)}, u32[]{:S(2)}) %collective-permute-start.9) | collective-permute-done | bytes 524320 | tf_op jit(solution)/shard_map/ppermute | solution.py:287
  88.7 1.8 %collective-permute-start.10 = (bf16[2,512,128]{2,1,0:T(8,128)(2,1)S(1)}, bf16[2,512,128]{2,1,0:T(8,128)(2,1)S(1)}, u32[]{:S(2)}, u32[]{:S(2)}) collective-permute-start(bf16[2,512,128]{2,1,0:T(8,128)(2,1)S(1)} %add_convert_fusion.8), channel_id=1, source_target_pairs={{2,4},{4,2},{6,0},{0,6},{3,5},{5,3},{7,1},{1,7},{10,12},{12,10},{1... | collective-permute-start | bytes 786440 | tf_op jit(solution)/shard_map/ppermute | solution.py:287
  90.7 1.1 collective-permute-start.4
  91.9 3.3 %collective-permute-done.10 = bf16[2,512,128]{2,1,0:T(8,128)(2,1)S(1)} collective-permute-done((bf16[2,512,128]{2,1,0:T(8,128)(2,1)S(1)}, bf16[2,512,128]{2,1,0:T(8,128)(2,1)S(1)}, u32[]{:S(2)}, u32[]{:S(2)}) %collective-permute-start.10) | collective-permute-done | bytes 262176 | tf_op jit(solution)/shard_map/ppermute | solution.py:287
  95.4 2.6 %collective-permute-start.11 = (bf16[1,512,128]{2,1,0:T(8,128)(2,1)S(1)}, bf16[1,512,128]{2,1,0:T(8,128)(2,1)S(1)}, u32[]{:S(2)}, u32[]{:S(2)}) collective-permute-start(bf16[1,512,128]{2,1,0:T(8,128)(2,1)S(1)} %add_convert_fusion.12), channel_id=1, source_target_pairs={{64,128},{128,64},{192,0},{0,192},{65,129},{129,65},{193,1},{1,193... | collective-permute-start | bytes 393224 | tf_op jit(solution)/shard_map/ppermute | solution.py:287
  98.0 0.4 collective-permute-start.5
  98.4 3.8 %collective-permute-done.11 = bf16[1,512,128]{2,1,0:T(8,128)(2,1)S(1)} collective-permute-done((bf16[1,512,128]{2,1,0:T(8,128)(2,1)S(1)}, bf16[1,512,128]{2,1,0:T(8,128)(2,1)S(1)}, u32[]{:S(2)}, u32[]{:S(2)}) %collective-permute-start.11) | collective-permute-done | bytes 131104 | tf_op jit(solution)/shard_map/ppermute | solution.py:287
  102.3 1.1 collective-permute-done.5
  103.5 1.6 %tail.1 = (f32[179,128]{1,0:T(8,128)S(1)}, bf16[4,128,128]{2,1,0:T(8,128)(2,1)S(1)}, bf16[4,128,128]{2,1,0:T(8,128)(2,1)S(1)}, bf16[4,128,128]{2,1,0:T(8,128)(2,...) custom-call(s32[1,179]{1,0:T(1,128)S(1)} %copy-done.3, ...), custom_call_target="tpu_custom_call" | custom-call | tf_op jit(solution)/shard_map/tail/pallas_call | solution.py:191
  105.2 0.7 adam.1
  105.9 6.8 %collective-permute-start.24 = (bf16[179,128]{1,0:T(8,128)(2,1)S(1)}, bf16[179,128]{1,0:T(8,128)(2,1)S(1)}, u32[]{:S(2)}, u32[]{:S(2)}) collective-permute-start(bf16[179,128]{1,0:T(8,128)(2,1)S(1)} %get-tuple-element.50.a_ref), channel_id=1, source_target_pairs={{0,1},{1,0},{2,3},{3,2},{4,5},{5,4},{6,7},{7,6},{8,9},{9,8},{10,11... | collective-permute-start | bytes 137480 | tf_op jit(solution)/shard_map/ppermute | solution.py:287
  112.7 0.9 collective-permute-done.24.b_ref
  113.7 1.1 collective-permute-start.27
  114.7 3.0 %collective-permute-start.28 = (bf16[4,128,128]{2,1,0:T(8,128)(2,1)S(1)}, bf16[4,128,128]{2,1,0:T(8,128)(2,1)S(1)}, u32[]{:S(2)}, u32[]{:S(2)}) collective-permute-start(bf16[4,128,128]{2,1,0:T(8,128)(2,1)S(1)} %get-tuple-element.53), channel_id=1, source_target_pairs={{0,16},{8,24},{16,32},{24,40},{32,48},{40,56},{48,0},{56,8},{1,17}... | collective-permute-start | bytes 393224 | tf_op jit(solution)/shard_map/ppermute | solution.py:287
  117.7 3.8 %collective-permute-start.29 = (bf16[4,128,128]{2,1,0:T(8,128)(2,1)S(1)}, bf16[4,128,128]{2,1,0:T(8,128)(2,1)S(1)}, u32[]{:S(2)}, u32[]{:S(2)}) collective-permute-start(bf16[4,128,128]{2,1,0:T(8,128)(2,1)S(1)} %get-tuple-element.54), channel_id=1, source_target_pairs={{0,24},{8,32},{16,40},{24,48},{32,56},{40,0},{48,8},{56,16},{1,25}... | collective-permute-start | bytes 393224 | tf_op jit(solution)/shard_map/ppermute | solution.py:287
  121.5 1.6 %collective-permute-start.26 = (bf16[4,179,128]{2,1,0:T(8,128)(2,1)S(1)}, bf16[4,179,128]{2,1,0:T(8,128)(2,1)S(1)}, u32[]{:S(2)}, u32[]{:S(2)}) collective-permute-start(bf16[4,179,128]{2,1,0:T(8,128)(2,1)S(1)} %pad_maximum_fusion), channel_id=1, source_target_pairs={{2,4},{4,2},{6,0},{0,6},{3,5},{5,3},{7,1},{1,7},{10,12},{12,10},{1... | collective-permute-start | bytes 549896 | tf_op jit(solution)/shard_map/ppermute | solution.py:287
  123.1 2.3 %collective-permute-start.30 = (bf16[4,128,128]{2,1,0:T(8,128)(2,1)S(1)}, bf16[4,128,128]{2,1,0:T(8,128)(2,1)S(1)}, u32[]{:S(2)}, u32[]{:S(2)}) collective-permute-start(bf16[4,128,128]{2,1,0:T(8,128)(2,1)S(1)} %get-tuple-element.55), channel_id=1, source_target_pairs={{0,32},{8,40},{16,48},{24,56},{32,0},{40,8},{48,16},{56,24},{1,33}... | collective-permute-start | bytes 393224 | tf_op jit(solution)/shard_map/ppermute | solution.py:287
  125.5 2.6 %collective-permute-start.31 = (bf16[4,128,128]{2,1,0:T(8,128)(2,1)S(1)}, bf16[4,128,128]{2,1,0:T(8,128)(2,1)S(1)}, u32[]{:S(2)}, u32[]{:S(2)}) collective-permute-start(bf16[4,128,128]{2,1,0:T(8,128)(2,1)S(1)} %get-tuple-element.56), channel_id=1, source_target_pairs={{0,40},{8,48},{16,56},{24,0},{32,8},{40,16},{48,24},{56,32},{1,41}... | collective-permute-start | bytes 393224 | tf_op jit(solution)/shard_map/ppermute | solution.py:287
  128.1 2.4 %collective-permute-start.32 = (bf16[4,128,128]{2,1,0:T(8,128)(2,1)S(1)}, bf16[4,128,128]{2,1,0:T(8,128)(2,1)S(1)}, u32[]{:S(2)}, u32[]{:S(2)}) collective-permute-start(bf16[4,128,128]{2,1,0:T(8,128)(2,1)S(1)} %get-tuple-element.57), channel_id=1, source_target_pairs={{0,48},{8,56},{16,0},{24,8},{32,16},{40,24},{48,32},{56,40},{1,49}... | collective-permute-start | bytes 393224 | tf_op jit(solution)/shard_map/ppermute | solution.py:287
  130.4 7.7 %collective-permute-done.29.refs_3_ = bf16[4,128,128]{2,1,0:T(8,128)(2,1)S(1)} collective-permute-done((bf16[4,128,128]{2,1,0:T(8,128)(2,1)S(1)}, bf16[4,128,128]{2,1,0:T(8,128)(2,1)S(1)}, u32[]{:S(2)}, u32[]{:S(2)}) %collective-permute-start.29) | collective-permute-done | bytes 131104 | tf_op jit(solution)/shard_map/ppermute | solution.py:287
  138.1 0.6 collective-permute-done.30.refs_4_
  138.8 1.8 %collective-permute-done.31.refs_5_ = bf16[4,128,128]{2,1,0:T(8,128)(2,1)S(1)} collective-permute-done((bf16[4,128,128]{2,1,0:T(8,128)(2,1)S(1)}, bf16[4,128,128]{2,1,0:T(8,128)(2,1)S(1)}, u32[]{:S(2)}, u32[]{:S(2)}) %collective-permute-start.31) | collective-permute-done | bytes 131104 | tf_op jit(solution)/shard_map/ppermute | solution.py:287
  140.6 7.5 %collective-permute-done.32.refs_6_ = bf16[4,128,128]{2,1,0:T(8,128)(2,1)S(1)} collective-permute-done((bf16[4,128,128]{2,1,0:T(8,128)(2,1)S(1)}, bf16[4,128,128]{2,1,0:T(8,128)(2,1)S(1)}, u32[]{:S(2)}, u32[]{:S(2)}) %collective-permute-start.32) | collective-permute-done | bytes 131104 | tf_op jit(solution)/shard_map/ppermute | solution.py:287
  148.1 0.9 collective-permute-done.33.refs_7_
  149.0 1.8 %join.1 = (bf16[179,1024]{1,0:T(8,128)(2,1)}, bf16[32,128,128]{2,1,0:T(8,128)(2,1)}) custom-call(bf16[179,128]{1,0:T(8,128)(2,1)S(1)} %get-tuple-element.50.a_ref, bf16[179,128]{1,0:T(8,128)(2,1)S(1)} %collective-permute-done.24.b_ref, bf16[2,179,128]{2,1,0:T(8,128)(2,1)S(1)} %collective-permute-done.25.c_ref, ...), custom_call_target="tpu_custom_call" | custom-call | tf_op jit(solution)/shard_map/join/pallas_call | solution.py:257
  (52 shorter events, 2.1 us)
Async XLA Ops:
  5.9 18.0 %collective-permute-start.13 = (bf16[8,384,128]{2,1,0:T(8,128)(2,1)S(1)}, bf16[8,384,128]{2,1,0:T(8,128)(2,1)S(1)}, u32[]{:S(2)}, u32[]{:S(2)}) collective-permute-start(bf16[8,384,128]{2,1,0:T(8,128)(2,1)S(1)} %mm.20), channel_id=1, source_target_pairs={{0,1},{1,0},{2,3},{3,2},{4,5},{5,4},{6,7},{7,6},{8,9},{9,8},{10,11... | collective-permute-start | bytes 2359304 | tf_op jit(solution)/shard_map/ppermute | solution.py:287
  10.1 18.4 %collective-permute-start.19 = (bf16[8,400,128]{2,1,0:T(8,128)(2,1)S(1)}, bf16[8,400,128]{2,1,0:T(8,128)(2,1)S(1)}, u32[]{:S(2)}, u32[]{:S(2)}) collective-permute-start(bf16[8,400,128]{2,1,0:T(8,128)(2,1)S(1)} %mm.23), channel_id=1, source_target_pairs={{0,1},{1,0},{2,3},{3,2},{4,5},{5,4},{6,7},{7,6},{8,9},{9,8},{10,11... | collective-permute-start | bytes 2457608 | tf_op jit(solution)/shard_map/ppermute | solution.py:287
  12.4 19.8 %collective-permute-start.12 = (bf16[8,384,128]{2,1,0:T(8,128)(2,1)S(1)}, bf16[8,384,128]{2,1,0:T(8,128)(2,1)S(1)}, u32[]{:S(2)}, u32[]{:S(2)}) collective-permute-start(bf16[8,384,128]{2,1,0:T(8,128)(2,1)S(1)} %get-tuple-element.42), channel_id=1, source_target_pairs={{0,1},{1,0},{2,3},{3,2},{4,5},{5,4},{6,7},{7,6},{8,9},{9,8},{10,11... | collective-permute-start | bytes 2359304 | tf_op jit(solution)/shard_map/ppermute | solution.py:287
  14.0 15.1 %collective-permute-start.7 = (bf16[8,512,128]{2,1,0:T(8,128)(2,1)S(1)}, bf16[8,512,128]{2,1,0:T(8,128)(2,1)S(1)}, u32[]{:S(2)}, u32[]{:S(2)}) collective-permute-start(bf16[8,512,128]{2,1,0:T(8,128)(2,1)S(1)} %mm.17), channel_id=1, source_target_pairs={{0,1},{1,0},{2,3},{3,2},{4,5},{5,4},{6,7},{7,6},{8,9},{9,8},{10,11... | collective-permute-start | bytes 3145736 | tf_op jit(solution)/shard_map/ppermute | solution.py:287
  15.3 29.4 %collective-permute-start.1 = (bf16[8,512,128]{2,1,0:T(8,128)(2,1)S(1)}, bf16[8,512,128]{2,1,0:T(8,128)(2,1)S(1)}, u32[]{:S(2)}, u32[]{:S(2)}) collective-permute-start(bf16[8,512,128]{2,1,0:T(8,128)(2,1)S(1)} %mm.14), channel_id=1, source_target_pairs={{0,1},{1,0},{2,3},{3,2},{4,5},{5,4},{6,7},{7,6},{8,9},{9,8},{10,11... | collective-permute-start | bytes 3145736 | tf_op jit(solution)/shard_map/ppermute | solution.py:287
  24.1 20.4 %collective-permute-start.14 = (bf16[8,384,128]{2,1,0:T(8,128)(2,1)S(1)}, bf16[8,384,128]{2,1,0:T(8,128)(2,1)S(1)}, u32[]{:S(2)}, u32[]{:S(2)}) collective-permute-start(bf16[8,384,128]{2,1,0:T(8,128)(2,1)S(1)} %add_convert_fusion.3), channel_id=1, source_target_pairs={{2,4},{4,2},{6,0},{0,6},{3,5},{5,3},{7,1},{1,7},{10,12},{12,10},{1... | collective-permute-start | bytes 2359304 | tf_op jit(solution)/shard_map/ppermute | solution.py:287
  28.5 18.0 %collective-permute-start.18 = (bf16[8,400,128]{2,1,0:T(8,128)(2,1)S(1)}, bf16[8,400,128]{2,1,0:T(8,128)(2,1)S(1)}, u32[]{:S(2)}, u32[]{:S(2)}) collective-permute-start(bf16[8,400,128]{2,1,0:T(8,128)(2,1)S(1)} %get-tuple-element.45), channel_id=1, source_target_pairs={{0,1},{1,0},{2,3},{3,2},{4,5},{5,4},{6,7},{7,6},{8,9},{9,8},{10,11... | collective-permute-start | bytes 2457608 | tf_op jit(solution)/shard_map/ppermute | solution.py:287
  29.1 21.0 %collective-permute-start.20 = (bf16[8,400,128]{2,1,0:T(8,128)(2,1)S(1)}, bf16[8,400,128]{2,1,0:T(8,128)(2,1)S(1)}, u32[]{:S(2)}, u32[]{:S(2)}) collective-permute-start(bf16[8,400,128]{2,1,0:T(8,128)(2,1)S(1)} %add_convert_fusion.2), channel_id=1, source_target_pairs={{64,128},{128,64},{192,0},{0,192},{65,129},{129,65},{193,1},{1,193... | collective-permute-start | bytes 2457608 | tf_op jit(solution)/shard_map/ppermute | solution.py:287
  32.2 37.6 %collective-permute-start.6 = (bf16[8,512,128]{2,1,0:T(8,128)(2,1)S(1)}, bf16[8,512,128]{2,1,0:T(8,128)(2,1)S(1)}, u32[]{:S(2)}, u32[]{:S(2)}) collective-permute-start(bf16[8,512,128]{2,1,0:T(8,128)(2,1)S(1)} %get-tuple-element.39), channel_id=1, source_target_pairs={{0,1},{1,0},{2,3},{3,2},{4,5},{5,4},{6,7},{7,6},{8,9},{9,8},{10,11... | collective-permute-start | bytes 3145736 | tf_op jit(solution)/shard_map/ppermute | solution.py:287
  44.5 25.4 %collective-permute-start.8 = (bf16[8,512,128]{2,1,0:T(8,128)(2,1)S(1)}, bf16[8,512,128]{2,1,0:T(8,128)(2,1)S(1)}, u32[]{:S(2)}, u32[]{:S(2)}) collective-permute-start(bf16[8,512,128]{2,1,0:T(8,128)(2,1)S(1)} %add_convert_fusion), channel_id=1, source_target_pairs={{0,64},{64,0},{128,192},{192,128},{1,65},{65,1},{129,193},{193,129... | collective-permute-start | bytes 3145736 | tf_op jit(solution)/shard_map/ppermute | solution.py:287
  44.7 13.8 %collective-permute-start.15 = (bf16[4,384,128]{2,1,0:T(8,128)(2,1)S(1)}, bf16[4,384,128]{2,1,0:T(8,128)(2,1)S(1)}, u32[]{:S(2)}, u32[]{:S(2)}) collective-permute-start(bf16[4,384,128]{2,1,0:T(8,128)(2,1)S(1)} %add_convert_fusion.7), channel_id=1, source_target_pairs={{64,128},{128,64},{192,0},{0,192},{65,129},{129,65},{193,1},{1,193... | collective-permute-start | bytes 1179656 | tf_op jit(solution)/shard_map/ppermute | solution.py:287
  46.5 25.2 %collective-permute-start = (bf16[8,512,128]{2,1,0:T(8,128)(2,1)S(1)}, bf16[8,512,128]{2,1,0:T(8,128)(2,1)S(1)}, u32[]{:S(2)}, u32[]{:S(2)}) collective-permute-start(bf16[8,512,128]{2,1,0:T(8,128)(2,1)S(1)} %get-tuple-element.36), channel_id=1, source_target_pairs={{0,1},{1,0},{2,3},{3,2},{4,5},{5,4},{6,7},{7,6},{8,9},{9,8},{10,11... | collective-permute-start | bytes 3145736 | tf_op jit(solution)/shard_map/ppermute | solution.py:287
  50.1 23.0 %collective-permute-start.2 = (bf16[8,512,128]{2,1,0:T(8,128)(2,1)S(1)}, bf16[8,512,128]{2,1,0:T(8,128)(2,1)S(1)}, u32[]{:S(2)}, u32[]{:S(2)}) collective-permute-start(bf16[8,512,128]{2,1,0:T(8,128)(2,1)S(1)} %add_convert_fusion.1), channel_id=1, source_target_pairs={{0,2},{2,0},{4,6},{6,4},{1,3},{3,1},{5,7},{7,5},{8,10},{10,8},{12,... | collective-permute-start | bytes 3145736 | tf_op jit(solution)/shard_map/ppermute | solution.py:287
  58.5 11.2 %collective-permute-start.21 = (bf16[4,400,128]{2,1,0:T(8,128)(2,1)S(1)}, bf16[4,400,128]{2,1,0:T(8,128)(2,1)S(1)}, u32[]{:S(2)}, u32[]{:S(2)}) collective-permute-start(bf16[4,400,128]{2,1,0:T(8,128)(2,1)S(1)} %add_convert_fusion.6), channel_id=1, source_target_pairs={{2,4},{4,2},{6,0},{0,6},{3,5},{5,3},{7,1},{1,7},{10,12},{12,10},{1... | collective-permute-start | bytes 1228808 | tf_op jit(solution)/shard_map/ppermute | solution.py:287
  69.7 7.6 %collective-permute-start.16 = (bf16[2,384,128]{2,1,0:T(8,128)(2,1)S(1)}, bf16[2,384,128]{2,1,0:T(8,128)(2,1)S(1)}, u32[]{:S(2)}, u32[]{:S(2)}) collective-permute-start(bf16[2,384,128]{2,1,0:T(8,128)(2,1)S(1)} %add_convert_fusion.11), channel_id=1, source_target_pairs={{0,2},{2,0},{4,6},{6,4},{1,3},{3,1},{5,7},{7,5},{8,10},{10,8},{12,... | collective-permute-start | bytes 589832 | tf_op jit(solution)/shard_map/ppermute | solution.py:287
  69.8 7.7 %collective-permute-start.22 = (bf16[2,400,128]{2,1,0:T(8,128)(2,1)S(1)}, bf16[2,400,128]{2,1,0:T(8,128)(2,1)S(1)}, u32[]{:S(2)}, u32[]{:S(2)}) collective-permute-start(bf16[2,400,128]{2,1,0:T(8,128)(2,1)S(1)} %add_convert_fusion.10), channel_id=1, source_target_pairs={{0,64},{64,0},{128,192},{192,128},{1,65},{65,1},{129,193},{193,129... | collective-permute-start | bytes 614408 | tf_op jit(solution)/shard_map/ppermute | solution.py:287
  70.2 18.4 %collective-permute-start.9 = (bf16[4,512,128]{2,1,0:T(8,128)(2,1)S(1)}, bf16[4,512,128]{2,1,0:T(8,128)(2,1)S(1)}, u32[]{:S(2)}, u32[]{:S(2)}) collective-permute-start(bf16[4,512,128]{2,1,0:T(8,128)(2,1)S(1)} %add_convert_fusion.4), channel_id=1, source_target_pairs={{0,2},{2,0},{4,6},{6,4},{1,3},{3,1},{5,7},{7,5},{8,10},{10,8},{12,... | collective-permute-start | bytes 1572872 | tf_op jit(solution)/shard_map/ppermute | solution.py:287
  73.3 17.2 %collective-permute-start.3 = (bf16[4,512,128]{2,1,0:T(8,128)(2,1)S(1)}, bf16[4,512,128]{2,1,0:T(8,128)(2,1)S(1)}, u32[]{:S(2)}, u32[]{:S(2)}) collective-permute-start(bf16[4,512,128]{2,1,0:T(8,128)(2,1)S(1)} %add_convert_fusion.5), channel_id=1, source_target_pairs={{0,64},{64,0},{128,192},{192,128},{1,65},{65,1},{129,193},{193,129... | collective-permute-start | bytes 1572872 | tf_op jit(solution)/shard_map/ppermute | solution.py:287
  77.4 9.0 %collective-permute-start.17 = (bf16[1,384,128]{2,1,0:T(8,128)(2,1)S(1)}, bf16[1,384,128]{2,1,0:T(8,128)(2,1)S(1)}, u32[]{:S(2)}, u32[]{:S(2)}) collective-permute-start(bf16[1,384,128]{2,1,0:T(8,128)(2,1)S(1)} %add_convert_fusion.15), channel_id=1, source_target_pairs={{0,64},{64,0},{128,192},{192,128},{1,65},{65,1},{129,193},{193,129... | collective-permute-start | bytes 294920 | tf_op jit(solution)/shard_map/ppermute | solution.py:287
  77.6 14.2 %collective-permute-start.23 = (bf16[1,400,128]{2,1,0:T(8,128)(2,1)S(1)}, bf16[1,400,128]{2,1,0:T(8,128)(2,1)S(1)}, u32[]{:S(2)}, u32[]{:S(2)}) collective-permute-start(bf16[1,400,128]{2,1,0:T(8,128)(2,1)S(1)} %add_convert_fusion.14), channel_id=1, source_target_pairs={{0,2},{2,0},{4,6},{6,4},{1,3},{3,1},{5,7},{7,5},{8,10},{10,8},{12,... | collective-permute-start | bytes 307208 | tf_op jit(solution)/shard_map/ppermute | solution.py:287
  88.7 6.5 %collective-permute-start.10 = (bf16[2,512,128]{2,1,0:T(8,128)(2,1)S(1)}, bf16[2,512,128]{2,1,0:T(8,128)(2,1)S(1)}, u32[]{:S(2)}, u32[]{:S(2)}) collective-permute-start(bf16[2,512,128]{2,1,0:T(8,128)(2,1)S(1)} %add_convert_fusion.8), channel_id=1, source_target_pairs={{2,4},{4,2},{6,0},{0,6},{3,5},{5,3},{7,1},{1,7},{10,12},{12,10},{1... | collective-permute-start | bytes 786440 | tf_op jit(solution)/shard_map/ppermute | solution.py:287
  90.7 12.8 %copy-start.3 = (s32[1,179]{1,0:T(1,128)S(1)}, s32[1,179]{1,0:T(1,128)}, u32[]{:S(2)}) copy-start(s32[1,179]{1,0:T(1,128)} %ids_ref.1) | copy-start | bytes 2152
  90.7 12.8 %copy-start.4 = (s32[14,1]{0,1:T(1,128)S(1)}, s32[14,1]{0,1:T(1,128)}, u32[]{:S(2)}) copy-start(s32[14,1]{0,1:T(1,128)} %param.12) | copy-start | bytes 172
  90.7 7.2 %collective-permute-start.4 = (bf16[2,512,128]{2,1,0:T(8,128)(2,1)S(1)}, bf16[2,512,128]{2,1,0:T(8,128)(2,1)S(1)}, u32[]{:S(2)}, u32[]{:S(2)}) collective-permute-start(bf16[2,512,128]{2,1,0:T(8,128)(2,1)S(1)} %add_convert_fusion.9), channel_id=1, source_target_pairs={{64,128},{128,64},{192,0},{0,192},{65,129},{129,65},{193,1},{1,193... | collective-permute-start | bytes 786440 | tf_op jit(solution)/shard_map/ppermute | solution.py:287
  95.3 9.8 %copy-start = (f32[179,128]{1,0:T(8,128)S(1)}, f32[179,128]{1,0:T(8,128)}, u32[]{:S(2)}) copy-start(f32[179,128]{1,0:T(8,128)} %ma_ref.1) | copy-start | bytes 274948
  95.3 9.8 %copy-start.1 = (f32[179,128]{1,0:T(8,128)S(1)}, f32[179,128]{1,0:T(8,128)}, u32[]{:S(2)}) copy-start(f32[179,128]{1,0:T(8,128)} %mo_ref.1) | copy-start | bytes 274948
  95.4 9.8 %copy-start.2 = (f32[179,128]{1,0:T(8,128)S(1)}, f32[179,128]{1,0:T(8,128)}, u32[]{:S(2)}) copy-start(f32[179,128]{1,0:T(8,128)} %se_ref.1) | copy-start | bytes 274948
  95.4 6.8 %collective-permute-start.11 = (bf16[1,512,128]{2,1,0:T(8,128)(2,1)S(1)}, bf16[1,512,128]{2,1,0:T(8,128)(2,1)S(1)}, u32[]{:S(2)}, u32[]{:S(2)}) collective-permute-start(bf16[1,512,128]{2,1,0:T(8,128)(2,1)S(1)} %add_convert_fusion.12), channel_id=1, source_target_pairs={{64,128},{128,64},{192,0},{0,192},{65,129},{129,65},{193,1},{1,193... | collective-permute-start | bytes 393224 | tf_op jit(solution)/shard_map/ppermute | solution.py:287
  98.0 5.4 %collective-permute-start.5 = (bf16[1,512,128]{2,1,0:T(8,128)(2,1)S(1)}, bf16[1,512,128]{2,1,0:T(8,128)(2,1)S(1)}, u32[]{:S(2)}, u32[]{:S(2)}) collective-permute-start(bf16[1,512,128]{2,1,0:T(8,128)(2,1)S(1)} %add_convert_fusion.13), channel_id=1, source_target_pairs={{2,4},{4,2},{6,0},{0,6},{3,5},{5,3},{7,1},{1,7},{10,12},{12,10},{1... | collective-permute-start | bytes 393224 | tf_op jit(solution)/shard_map/ppermute | solution.py:287
  105.9 7.6 %collective-permute-start.24 = (bf16[179,128]{1,0:T(8,128)(2,1)S(1)}, bf16[179,128]{1,0:T(8,128)(2,1)S(1)}, u32[]{:S(2)}, u32[]{:S(2)}) collective-permute-start(bf16[179,128]{1,0:T(8,128)(2,1)S(1)} %get-tuple-element.50.a_ref), channel_id=1, source_target_pairs={{0,1},{1,0},{2,3},{3,2},{4,5},{5,4},{6,7},{7,6},{8,9},{9,8},{10,11... | collective-permute-start | bytes 137480 | tf_op jit(solution)/shard_map/ppermute | solution.py:287
  113.6 7.9 %collective-permute-start.25 = (bf16[2,179,128]{2,1,0:T(8,128)(2,1)S(1)}, bf16[2,179,128]{2,1,0:T(8,128)(2,1)S(1)}, u32[]{:S(2)}, u32[]{:S(2)}) collective-permute-start(bf16[2,179,128]{2,1,0:T(8,128)(2,1)S(1)} %pad_maximum_fusion.1), channel_id=1, source_target_pairs={{0,2},{2,0},{4,6},{6,4},{1,3},{3,1},{5,7},{7,5},{8,10},{10,8},{12,... | collective-permute-start | bytes 274952 | tf_op jit(solution)/shard_map/ppermute | solution.py:287
  113.7 11.8 %collective-permute-start.27 = (bf16[4,128,128]{2,1,0:T(8,128)(2,1)S(1)}, bf16[4,128,128]{2,1,0:T(8,128)(2,1)S(1)}, u32[]{:S(2)}, u32[]{:S(2)}) collective-permute-start(bf16[4,128,128]{2,1,0:T(8,128)(2,1)S(1)} %get-tuple-element.52), channel_id=1, source_target_pairs={{0,8},{8,16},{16,24},{24,32},{32,40},{40,48},{48,56},{56,0},{1,9},... | collective-permute-start | bytes 393224 | tf_op jit(solution)/shard_map/ppermute | solution.py:287
  114.7 13.3 %collective-permute-start.28 = (bf16[4,128,128]{2,1,0:T(8,128)(2,1)S(1)}, bf16[4,128,128]{2,1,0:T(8,128)(2,1)S(1)}, u32[]{:S(2)}, u32[]{:S(2)}) collective-permute-start(bf16[4,128,128]{2,1,0:T(8,128)(2,1)S(1)} %get-tuple-element.53), channel_id=1, source_target_pairs={{0,16},{8,24},{16,32},{24,40},{32,48},{40,56},{48,0},{56,8},{1,17}... | collective-permute-start | bytes 393224 | tf_op jit(solution)/shard_map/ppermute | solution.py:287
  117.7 20.4 %collective-permute-start.29 = (bf16[4,128,128]{2,1,0:T(8,128)(2,1)S(1)}, bf16[4,128,128]{2,1,0:T(8,128)(2,1)S(1)}, u32[]{:S(2)}, u32[]{:S(2)}) collective-permute-start(bf16[4,128,128]{2,1,0:T(8,128)(2,1)S(1)} %get-tuple-element.54), channel_id=1, source_target_pairs={{0,24},{8,32},{16,40},{24,48},{32,56},{40,0},{48,8},{56,16},{1,25}... | collective-permute-start | bytes 393224 | tf_op jit(solution)/shard_map/ppermute | solution.py:287
  121.5 27.5 %collective-permute-start.26 = (bf16[4,179,128]{2,1,0:T(8,128)(2,1)S(1)}, bf16[4,179,128]{2,1,0:T(8,128)(2,1)S(1)}, u32[]{:S(2)}, u32[]{:S(2)}) collective-permute-start(bf16[4,179,128]{2,1,0:T(8,128)(2,1)S(1)} %pad_maximum_fusion), channel_id=1, source_target_pairs={{2,4},{4,2},{6,0},{0,6},{3,5},{5,3},{7,1},{1,7},{10,12},{12,10},{1... | collective-permute-start | bytes 549896 | tf_op jit(solution)/shard_map/ppermute | solution.py:287
  123.1 15.6 %collective-permute-start.30 = (bf16[4,128,128]{2,1,0:T(8,128)(2,1)S(1)}, bf16[4,128,128]{2,1,0:T(8,128)(2,1)S(1)}, u32[]{:S(2)}, u32[]{:S(2)}) collective-permute-start(bf16[4,128,128]{2,1,0:T(8,128)(2,1)S(1)} %get-tuple-element.55), channel_id=1, source_target_pairs={{0,32},{8,40},{16,48},{24,56},{32,0},{40,8},{48,16},{56,24},{1,33}... | collective-permute-start | bytes 393224 | tf_op jit(solution)/shard_map/ppermute | solution.py:287
  125.5 15.1 %collective-permute-start.31 = (bf16[4,128,128]{2,1,0:T(8,128)(2,1)S(1)}, bf16[4,128,128]{2,1,0:T(8,128)(2,1)S(1)}, u32[]{:S(2)}, u32[]{:S(2)}) collective-permute-start(bf16[4,128,128]{2,1,0:T(8,128)(2,1)S(1)} %get-tuple-element.56), channel_id=1, source_target_pairs={{0,40},{8,48},{16,56},{24,0},{32,8},{40,16},{48,24},{56,32},{1,41}... | collective-permute-start | bytes 393224 | tf_op jit(solution)/shard_map/ppermute | solution.py:287
  128.1 20.0 %collective-permute-start.32 = (bf16[4,128,128]{2,1,0:T(8,128)(2,1)S(1)}, bf16[4,128,128]{2,1,0:T(8,128)(2,1)S(1)}, u32[]{:S(2)}, u32[]{:S(2)}) collective-permute-start(bf16[4,128,128]{2,1,0:T(8,128)(2,1)S(1)} %get-tuple-element.57), channel_id=1, source_target_pairs={{0,48},{8,56},{16,0},{24,8},{32,16},{40,24},{48,32},{56,40},{1,49}... | collective-permute-start | bytes 393224 | tf_op jit(solution)/shard_map/ppermute | solution.py:287
  138.1 10.8 %collective-permute-start.33 = (bf16[4,128,128]{2,1,0:T(8,128)(2,1)S(1)}, bf16[4,128,128]{2,1,0:T(8,128)(2,1)S(1)}, u32[]{:S(2)}, u32[]{:S(2)}) collective-permute-start(bf16[4,128,128]{2,1,0:T(8,128)(2,1)S(1)} %get-tuple-element.58), channel_id=1, source_target_pairs={{0,56},{8,0},{16,8},{24,16},{32,24},{40,32},{48,40},{56,48},{1,57}... | collective-permute-start | bytes 393224 | tf_op jit(solution)/shard_map/ppermute | solution.py:287

commit v2 on v1

--- a/solution.py
+++ b/solution.py
@@ -164,19 +164,22 @@
     pack[...] = jnp.zeros_like(pack)
 
     def take(i, _):
-        h = ids_ref[0, i]
-        hot_ref[pl.ds(i, 1), :] = acc[pl.ds(h, 1), :] * scale
-        acc[pl.ds(h, 1), :] = jnp.zeros((1, CB), jnp.float32)
+        hot_ref[pl.ds(i, 1), :] = acc[pl.ds(ids_ref[0, i], 1), :] * scale
         return 0
 
-    lax.fori_loop(0, hot_ref.shape[0], take, 0, unroll=4)
+    def clear(i, _):
+        acc[pl.ds(ids_ref[0, i], 1), :] = jnp.zeros((1, CB), jnp.float32)
+        return 0
+
+    lax.fori_loop(0, hot_ref.shape[0], take, 0, unroll=16)
+    lax.fori_loop(0, hot_ref.shape[0], clear, 0, unroll=16)
     for b in range(acc.shape[0] // CB):
         x = acc[b * CB : (b + 1) * CB, :] * scale
         owner = own_ref[b]
         slot = jnp.int32(0)
         for e in range(b):
             slot += (own_ref[e] == owner).astype(jnp.int32)
-        pack[((owner - lax.axis_index("tensor")) & 7) * SLOTS + slot] = x.T.astype(jnp.bfloat16)
+        pack[((owner - lax.axis_index("tensor")) & 7) * SLOTS + slot] = x.astype(jnp.bfloat16).T
     for d in range(8):
         at = 0
         for e, lo, n in PACKS[d]:

time: 152 us -> 151 us (level)
  no operation moved by 1% of the time
where the time goes in v2:
time: 151 us
  waiting for transfers between devices  74.9 us (50%)
  starting transfers between devices  45.9 us (30%)
  Pallas kernels  25.1 us (17%)
  other arithmetic  2.91 us (2%)
  between operations  1.85 us (1%)
    ppermute x34, waiting for transfers between devices, moved(): return lax.ppermute(v, axis, pairs)  74.9 us
    ppermute x34, starting transfers between devices, moved(): return lax.ppermute(v, axis, pairs)  45.9 us
    pallas_call x12, Pallas kernels, product(): pl.pallas_call(functools.partial(mm_kernel, spare=spare, k=k, half=half,...  17.5 us
    pallas_call x1, Pallas kernels, loaded(): pl.pallas_call(load_kernel, grid_spec=pltpu.PrefetchScalarGridSpec(num_sc...  3.71 us
  transfers between devices with their start and end apart: 34, of which 17 were waited for; matrix products, arithmetic and copies ran while one was open for 2% of the time, Pallas kernels for 11%

profile of v2, /device:TPU:1, one launch (start us, length us, event | category | flops | bytes accessed | tf_op | source)
XLA Modules:
  0.0 150.7 jit_solution(9533603799026727425)
XLA Ops:
  1.3 3.7 %load.1 = (bf16[768,4096]{1,0:T(8,128)(2,1)S(1)}, bf16[512,768]{1,0:T(8,128)(2,1)S(1)}, bf16[512,768]{1,0:T(8,128)(2,1)S(1)}, bf16[384,768]{1,0:T(8,128)(2,1)S(1)}, bf16[384,768]{1,0:T(8,128)(2,1)S(1)}) custom-call(s32[1]{0:T(128)S(6)} %copy.13.cnt_ref, bf16[768,4096]{1,0:T(8,128)(2,1)} %a_hbm.1, bf16[768,1792]{1,0:T(8,128)(2,1)} %g_hbm.1), custom_call_target="tpu_custom_call" | custom-call | flops 2000000000 | tf_op jit(solution)/shard_map/load/pallas_call | solution.py:81
  5.0 0.9 mm.20
  5.9 3.3 %collective-permute-start.13 = (bf16[8,384,128]{2,1,0:T(8,128)(2,1)S(1)}, bf16[8,384,128]{2,1,0:T(8,128)(2,1)S(1)}, u32[]{:S(2)}, u32[]{:S(2)}) collective-permute-start(bf16[8,384,128]{2,1,0:T(8,128)(2,1)S(1)} %mm.20), channel_id=1, source_target_pairs={{0,1},{1,0},{2,3},{3,2},{4,5},{5,4},{6,7},{7,6},{8,9},{9,8},{10,11... | collective-permute-start | bytes 2359304 | tf_op jit(solution)/shard_map/ppermute | solution.py:290
  9.2 0.9 mm.23
  10.2 2.2 %mm.18 = (bf16[8,384,128]{2,1,0:T(8,128)(2,1)S(1)}, bf16[8,384,128]{2,1,0:T(8,128)(2,1)S(1)}) custom-call(s32[1]{0:T(128)S(6)} %copy.13.cnt_ref, bf16[384,768]{1,0:T(8,128)(2,1)S(1)} %get-tuple-element.40.l_ref, bf16[768,4096]{1,0:T(8,128)(2,1)S(1)} %get-tuple-element.34.a_ref), custom_call_target="tpu_custom_call" | custom-call | flops 1207959552 | tf_op jit(solution)/shard_map/mm/pallas_call | solution.py:138
  12.4 0.6 collective-permute-start.12
  13.0 1.0 mm.17
  14.2 1.1 mm.14
  15.3 0.7 collective-permute-start.1
  16.0 1.1 mm.16
  17.1 1.1 mm.13
  18.2 0.9 mm.19
  19.1 2.2 %mm.21 = (bf16[8,400,128]{2,1,0:T(8,128)(2,1)S(1)}, bf16[8,400,128]{2,1,0:T(8,128)(2,1)S(1)}) custom-call(s32[1]{0:T(128)S(6)} %copy.13.cnt_ref, bf16[384,768]{1,0:T(8,128)(2,1)S(1)} %get-tuple-element.43.l_ref, bf16[768,4096]{1,0:T(8,128)(2,1)S(1)} %get-tuple-element.34.a_ref), custom_call_target="tpu_custom_call" | custom-call | flops 1207959552 | tf_op jit(solution)/shard_map/mm/pallas_call | solution.py:138
  21.3 2.6 %mm.15 = (bf16[8,512,128]{2,1,0:T(8,128)(2,1)S(1)}, bf16[8,512,128]{2,1,0:T(8,128)(2,1)S(1)}) custom-call(s32[1]{0:T(128)S(6)} %copy.13.cnt_ref, bf16[512,768]{1,0:T(8,128)(2,1)S(1)} %get-tuple-element.37.l_ref, bf16[768,4096]{1,0:T(8,128)(2,1)S(1)} %get-tuple-element.34.a_ref), custom_call_target="tpu_custom_call" | custom-call | flops 1610612736 | tf_op jit(solution)/shard_map/mm/pallas_call | solution.py:138
  23.9 0.2 add_convert_fusion.3
  24.1 0.9 collective-permute-start.14
  25.0 0.9 mm.22
  25.9 2.6 %mm.12 = (bf16[8,512,128]{2,1,0:T(8,128)(2,1)S(1)}, bf16[8,512,128]{2,1,0:T(8,128)(2,1)S(1)}) custom-call(s32[1]{0:T(128)S(6)} %copy.13.cnt_ref, bf16[512,768]{1,0:T(8,128)(2,1)S(1)} %get-tuple-element.33.l_ref, bf16[768,4096]{1,0:T(8,128)(2,1)S(1)} %get-tuple-element.34.a_ref), custom_call_target="tpu_custom_call" | custom-call | flops 1610612736 | tf_op jit(solution)/shard_map/mm/pallas_call | solution.py:138
  28.5 0.4 collective-permute-start.18
  28.9 0.2 add_convert_fusion.2
  29.1 2.8 %collective-permute-start.20 = (bf16[8,400,128]{2,1,0:T(8,128)(2,1)S(1)}, bf16[8,400,128]{2,1,0:T(8,128)(2,1)S(1)}, u32[]{:S(2)}, u32[]{:S(2)}) collective-permute-start(bf16[8,400,128]{2,1,0:T(8,128)(2,1)S(1)} %add_convert_fusion.2), channel_id=1, source_target_pairs={{64,128},{128,64},{192,0},{0,192},{65,129},{129,65},{193,1},{1,193... | collective-permute-start | bytes 2457608 | tf_op jit(solution)/shard_map/ppermute | solution.py:290
  31.9 0.3 add_convert_fusion
  32.2 0.6 collective-permute-start.6
  32.8 11.7 %collective-permute-done.14 = bf16[8,384,128]{2,1,0:T(8,128)(2,1)S(1)} collective-permute-done((bf16[8,384,128]{2,1,0:T(8,128)(2,1)S(1)}, bf16[8,384,128]{2,1,0:T(8,128)(2,1)S(1)}, u32[]{:S(2)}, u32[]{:S(2)}) %collective-permute-start.14) | collective-permute-done | bytes 786464 | tf_op jit(solution)/shard_map/ppermute | solution.py:290
  44.5 0.2 add_convert_fusion.7
  44.7 1.6 %collective-permute-start.15 = (bf16[4,384,128]{2,1,0:T(8,128)(2,1)S(1)}, bf16[4,384,128]{2,1,0:T(8,128)(2,1)S(1)}, u32[]{:S(2)}, u32[]{:S(2)}) collective-permute-start(bf16[4,384,128]{2,1,0:T(8,128)(2,1)S(1)} %add_convert_fusion.7), channel_id=1, source_target_pairs={{64,128},{128,64},{192,0},{0,192},{65,129},{129,65},{193,1},{1,193... | collective-permute-start | bytes 1179656 | tf_op jit(solution)/shard_map/ppermute | solution.py:290
  46.3 0.3 add_convert_fusion.1
  46.5 1.5 %collective-permute-start = (bf16[8,512,128]{2,1,0:T(8,128)(2,1)S(1)}, bf16[8,512,128]{2,1,0:T(8,128)(2,1)S(1)}, u32[]{:S(2)}, u32[]{:S(2)}) collective-permute-start(bf16[8,512,128]{2,1,0:T(8,128)(2,1)S(1)} %get-tuple-element.36), channel_id=1, source_target_pairs={{0,1},{1,0},{2,3},{3,2},{4,5},{5,4},{6,7},{7,6},{8,9},{9,8},{10,11... | collective-permute-start | bytes 3145736 | tf_op jit(solution)/shard_map/ppermute | solution.py:290
  48.1 2.0 %collective-permute-done.20 = bf16[8,400,128]{2,1,0:T(8,128)(2,1)S(1)} collective-permute-done((bf16[8,400,128]{2,1,0:T(8,128)(2,1)S(1)}, bf16[8,400,128]{2,1,0:T(8,128)(2,1)S(1)}, u32[]{:S(2)}, u32[]{:S(2)}) %collective-permute-start.20) | collective-permute-done | bytes 819232 | tf_op jit(solution)/shard_map/ppermute | solution.py:290
  50.1 0.2 add_convert_fusion.6
  50.3 8.3 %collective-permute-done.15 = bf16[4,384,128]{2,1,0:T(8,128)(2,1)S(1)} collective-permute-done((bf16[4,384,128]{2,1,0:T(8,128)(2,1)S(1)}, bf16[4,384,128]{2,1,0:T(8,128)(2,1)S(1)}, u32[]{:S(2)}, u32[]{:S(2)}) %collective-permute-start.15) | collective-permute-done | bytes 393248 | tf_op jit(solution)/shard_map/ppermute | solution.py:290
  58.5 1.8 %collective-permute-start.21 = (bf16[4,400,128]{2,1,0:T(8,128)(2,1)S(1)}, bf16[4,400,128]{2,1,0:T(8,128)(2,1)S(1)}, u32[]{:S(2)}, u32[]{:S(2)}) collective-permute-start(bf16[4,400,128]{2,1,0:T(8,128)(2,1)S(1)} %add_convert_fusion.6), channel_id=1, source_target_pairs={{2,4},{4,2},{6,0},{0,6},{3,5},{5,3},{7,1},{1,7},{10,12},{12,10},{1... | collective-permute-start | bytes 1228808 | tf_op jit(solution)/shard_map/ppermute | solution.py:290
  60.4 9.3 %collective-permute-done.21 = bf16[4,400,128]{2,1,0:T(8,128)(2,1)S(1)} collective-permute-done((bf16[4,400,128]{2,1,0:T(8,128)(2,1)S(1)}, bf16[4,400,128]{2,1,0:T(8,128)(2,1)S(1)}, u32[]{:S(2)}, u32[]{:S(2)}) %collective-permute-start.21) | collective-permute-done | bytes 409632 | tf_op jit(solution)/shard_map/ppermute | solution.py:290
  70.0 0.2 add_convert_fusion.4
  70.2 1.5 %collective-permute-start.9 = (bf16[4,512,128]{2,1,0:T(8,128)(2,1)S(1)}, bf16[4,512,128]{2,1,0:T(8,128)(2,1)S(1)}, u32[]{:S(2)}, u32[]{:S(2)}) collective-permute-start(bf16[4,512,128]{2,1,0:T(8,128)(2,1)S(1)} %add_convert_fusion.4), channel_id=1, source_target_pairs={{0,2},{2,0},{4,6},{6,4},{1,3},{3,1},{5,7},{7,5},{8,10},{10,8},{12,... | collective-permute-start | bytes 1572872 | tf_op jit(solution)/shard_map/ppermute | solution.py:290
  71.7 1.4 collective-permute-done.2
  73.1 0.2 add_convert_fusion.5
  73.5 3.9 %collective-permute-done.16 = bf16[2,384,128]{2,1,0:T(8,128)(2,1)S(1)} collective-permute-done((bf16[2,384,128]{2,1,0:T(8,128)(2,1)S(1)}, bf16[2,384,128]{2,1,0:T(8,128)(2,1)S(1)}, u32[]{:S(2)}, u32[]{:S(2)}) %collective-permute-start.16) | collective-permute-done | bytes 196640 | tf_op jit(solution)/shard_map/ppermute | solution.py:290
  77.8 8.7 %collective-permute-done.17 = bf16[1,384,128]{2,1,0:T(8,128)(2,1)S(1)} collective-permute-done((bf16[1,384,128]{2,1,0:T(8,128)(2,1)S(1)}, bf16[1,384,128]{2,1,0:T(8,128)(2,1)S(1)}, u32[]{:S(2)}, u32[]{:S(2)}) %collective-permute-start.17) | collective-permute-done | bytes 98336 | tf_op jit(solution)/shard_map/ppermute | solution.py:290
  86.5 2.1 %collective-permute-done.9 = bf16[4,512,128]{2,1,0:T(8,128)(2,1)S(1)} collective-permute-done((bf16[4,512,128]{2,1,0:T(8,128)(2,1)S(1)}, bf16[4,512,128]{2,1,0:T(8,128)(2,1)S(1)}, u32[]{:S(2)}, u32[]{:S(2)}) %collective-permute-start.9) | collective-permute-done | bytes 524320 | tf_op jit(solution)/shard_map/ppermute | solution.py:290
  88.7 1.8 %collective-permute-start.10 = (bf16[2,512,128]{2,1,0:T(8,128)(2,1)S(1)}, bf16[2,512,128]{2,1,0:T(8,128)(2,1)S(1)}, u32[]{:S(2)}, u32[]{:S(2)}) collective-permute-start(bf16[2,512,128]{2,1,0:T(8,128)(2,1)S(1)} %add_convert_fusion.8), channel_id=1, source_target_pairs={{2,4},{4,2},{6,0},{0,6},{3,5},{5,3},{7,1},{1,7},{10,12},{12,10},{1... | collective-permute-start | bytes 786440 | tf_op jit(solution)/shard_map/ppermute | solution.py:290
  90.7 1.1 collective-permute-start.4
  91.9 3.3 %collective-permute-done.10 = bf16[2,512,128]{2,1,0:T(8,128)(2,1)S(1)} collective-permute-done((bf16[2,512,128]{2,1,0:T(8,128)(2,1)S(1)}, bf16[2,512,128]{2,1,0:T(8,128)(2,1)S(1)}, u32[]{:S(2)}, u32[]{:S(2)}) %collective-permute-start.10) | collective-permute-done | bytes 262176 | tf_op jit(solution)/shard_map/ppermute | solution.py:290
  95.4 2.6 %collective-permute-start.11 = (bf16[1,512,128]{2,1,0:T(8,128)(2,1)S(1)}, bf16[1,512,128]{2,1,0:T(8,128)(2,1)S(1)}, u32[]{:S(2)}, u32[]{:S(2)}) collective-permute-start(bf16[1,512,128]{2,1,0:T(8,128)(2,1)S(1)} %add_convert_fusion.12), channel_id=1, source_target_pairs={{64,128},{128,64},{192,0},{0,192},{65,129},{129,65},{193,1},{1,193... | collective-permute-start | bytes 393224 | tf_op jit(solution)/shard_map/ppermute | solution.py:290
  98.0 0.4 collective-permute-start.5
  98.4 3.8 %collective-permute-done.11 = bf16[1,512,128]{2,1,0:T(8,128)(2,1)S(1)} collective-permute-done((bf16[1,512,128]{2,1,0:T(8,128)(2,1)S(1)}, bf16[1,512,128]{2,1,0:T(8,128)(2,1)S(1)}, u32[]{:S(2)}, u32[]{:S(2)}) %collective-permute-start.11) | collective-permute-done | bytes 131104 | tf_op jit(solution)/shard_map/ppermute | solution.py:290
  102.3 1.1 collective-permute-done.5
  103.5 1.4 tail.1
  105.0 0.7 adam.1
  105.7 6.8 %collective-permute-start.24 = (bf16[179,128]{1,0:T(8,128)(2,1)S(1)}, bf16[179,128]{1,0:T(8,128)(2,1)S(1)}, u32[]{:S(2)}, u32[]{:S(2)}) collective-permute-start(bf16[179,128]{1,0:T(8,128)(2,1)S(1)} %get-tuple-element.50.a_ref), channel_id=1, source_target_pairs={{0,1},{1,0},{2,3},{3,2},{4,5},{5,4},{6,7},{7,6},{8,9},{9,8},{10,11... | collective-permute-start | bytes 137480 | tf_op jit(solution)/shard_map/ppermute | solution.py:290
  112.5 0.9 collective-permute-done.24.b_ref
  113.5 1.1 collective-permute-start.27
  114.5 3.0 %collective-permute-start.28 = (bf16[4,128,128]{2,1,0:T(8,128)(2,1)S(1)}, bf16[4,128,128]{2,1,0:T(8,128)(2,1)S(1)}, u32[]{:S(2)}, u32[]{:S(2)}) collective-permute-start(bf16[4,128,128]{2,1,0:T(8,128)(2,1)S(1)} %get-tuple-element.53), channel_id=1, source_target_pairs={{0,16},{8,24},{16,32},{24,40},{32,48},{40,56},{48,0},{56,8},{1,17}... | collective-permute-start | bytes 393224 | tf_op jit(solution)/shard_map/ppermute | solution.py:290
  117.5 3.8 %collective-permute-start.29 = (bf16[4,128,128]{2,1,0:T(8,128)(2,1)S(1)}, bf16[4,128,128]{2,1,0:T(8,128)(2,1)S(1)}, u32[]{:S(2)}, u32[]{:S(2)}) collective-permute-start(bf16[4,128,128]{2,1,0:T(8,128)(2,1)S(1)} %get-tuple-element.54), channel_id=1, source_target_pairs={{0,24},{8,32},{16,40},{24,48},{32,56},{40,0},{48,8},{56,16},{1,25}... | collective-permute-start | bytes 393224 | tf_op jit(solution)/shard_map/ppermute | solution.py:290
  121.3 1.6 %collective-permute-start.26 = (bf16[4,179,128]{2,1,0:T(8,128)(2,1)S(1)}, bf16[4,179,128]{2,1,0:T(8,128)(2,1)S(1)}, u32[]{:S(2)}, u32[]{:S(2)}) collective-permute-start(bf16[4,179,128]{2,1,0:T(8,128)(2,1)S(1)} %pad_maximum_fusion), channel_id=1, source_target_pairs={{2,4},{4,2},{6,0},{0,6},{3,5},{5,3},{7,1},{1,7},{10,12},{12,10},{1... | collective-permute-start | bytes 549896 | tf_op jit(solution)/shard_map/ppermute | solution.py:290
  122.9 2.3 %collective-permute-start.30 = (bf16[4,128,128]{2,1,0:T(8,128)(2,1)S(1)}, bf16[4,128,128]{2,1,0:T(8,128)(2,1)S(1)}, u32[]{:S(2)}, u32[]{:S(2)}) collective-permute-start(bf16[4,128,128]{2,1,0:T(8,128)(2,1)S(1)} %get-tuple-element.55), channel_id=1, source_target_pairs={{0,32},{8,40},{16,48},{24,56},{32,0},{40,8},{48,16},{56,24},{1,33}... | collective-permute-start | bytes 393224 | tf_op jit(solution)/shard_map/ppermute | solution.py:290
  125.3 2.6 %collective-permute-start.31 = (bf16[4,128,128]{2,1,0:T(8,128)(2,1)S(1)}, bf16[4,128,128]{2,1,0:T(8,128)(2,1)S(1)}, u32[]{:S(2)}, u32[]{:S(2)}) collective-permute-start(bf16[4,128,128]{2,1,0:T(8,128)(2,1)S(1)} %get-tuple-element.56), channel_id=1, source_target_pairs={{0,40},{8,48},{16,56},{24,0},{32,8},{40,16},{48,24},{56,32},{1,41}... | collective-permute-start | bytes 393224 | tf_op jit(solution)/shard_map/ppermute | solution.py:290
  127.9 2.4 %collective-permute-start.32 = (bf16[4,128,128]{2,1,0:T(8,128)(2,1)S(1)}, bf16[4,128,128]{2,1,0:T(8,128)(2,1)S(1)}, u32[]{:S(2)}, u32[]{:S(2)}) collective-permute-start(bf16[4,128,128]{2,1,0:T(8,128)(2,1)S(1)} %get-tuple-element.57), channel_id=1, source_target_pairs={{0,48},{8,56},{16,0},{24,8},{32,16},{40,24},{48,32},{56,40},{1,49}... | collective-permute-start | bytes 393224 | tf_op jit(solution)/shard_map/ppermute | solution.py:290
  130.2 7.7 %collective-permute-done.29.refs_3_ = bf16[4,128,128]{2,1,0:T(8,128)(2,1)S(1)} collective-permute-done((bf16[4,128,128]{2,1,0:T(8,128)(2,1)S(1)}, bf16[4,128,128]{2,1,0:T(8,128)(2,1)S(1)}, u32[]{:S(2)}, u32[]{:S(2)}) %collective-permute-start.29) | collective-permute-done | bytes 131104 | tf_op jit(solution)/shard_map/ppermute | solution.py:290
  137.9 0.6 collective-permute-done.30.refs_4_
  138.6 1.8 %collective-permute-done.31.refs_5_ = bf16[4,128,128]{2,1,0:T(8,128)(2,1)S(1)} collective-permute-done((bf16[4,128,128]{2,1,0:T(8,128)(2,1)S(1)}, bf16[4,128,128]{2,1,0:T(8,128)(2,1)S(1)}, u32[]{:S(2)}, u32[]{:S(2)}) %collective-permute-start.31) | collective-permute-done | bytes 131104 | tf_op jit(solution)/shard_map/ppermute | solution.py:290
  140.4 7.5 %collective-permute-done.32.refs_6_ = bf16[4,128,128]{2,1,0:T(8,128)(2,1)S(1)} collective-permute-done((bf16[4,128,128]{2,1,0:T(8,128)(2,1)S(1)}, bf16[4,128,128]{2,1,0:T(8,128)(2,1)S(1)}, u32[]{:S(2)}, u32[]{:S(2)}) %collective-permute-start.32) | collective-permute-done | bytes 131104 | tf_op jit(solution)/shard_map/ppermute | solution.py:290
  147.9 0.9 collective-permute-done.33.refs_7_
  148.8 1.8 %join.1 = (bf16[179,1024]{1,0:T(8,128)(2,1)}, bf16[32,128,128]{2,1,0:T(8,128)(2,1)}) custom-call(bf16[179,128]{1,0:T(8,128)(2,1)S(1)} %get-tuple-element.50.a_ref, bf16[179,128]{1,0:T(8,128)(2,1)S(1)} %collective-permute-done.24.b_ref, bf16[2,179,128]{2,1,0:T(8,128)(2,1)S(1)} %collective-permute-done.25.c_ref, ...), custom_call_target="tpu_custom_call" | custom-call | tf_op jit(solution)/shard_map/join/pallas_call | solution.py:260
  (52 shorter events, 2.1 us)
Async XLA Ops:
  5.9 18.0 %collective-permute-start.13 = (bf16[8,384,128]{2,1,0:T(8,128)(2,1)S(1)}, bf16[8,384,128]{2,1,0:T(8,128)(2,1)S(1)}, u32[]{:S(2)}, u32[]{:S(2)}) collective-permute-start(bf16[8,384,128]{2,1,0:T(8,128)(2,1)S(1)} %mm.20), channel_id=1, source_target_pairs={{0,1},{1,0},{2,3},{3,2},{4,5},{5,4},{6,7},{7,6},{8,9},{9,8},{10,11... | collective-permute-start | bytes 2359304 | tf_op jit(solution)/shard_map/ppermute | solution.py:290
  10.1 18.4 %collective-permute-start.19 = (bf16[8,400,128]{2,1,0:T(8,128)(2,1)S(1)}, bf16[8,400,128]{2,1,0:T(8,128)(2,1)S(1)}, u32[]{:S(2)}, u32[]{:S(2)}) collective-permute-start(bf16[8,400,128]{2,1,0:T(8,128)(2,1)S(1)} %mm.23), channel_id=1, source_target_pairs={{0,1},{1,0},{2,3},{3,2},{4,5},{5,4},{6,7},{7,6},{8,9},{9,8},{10,11... | collective-permute-start | bytes 2457608 | tf_op jit(solution)/shard_map/ppermute | solution.py:290
  12.4 19.8 %collective-permute-start.12 = (bf16[8,384,128]{2,1,0:T(8,128)(2,1)S(1)}, bf16[8,384,128]{2,1,0:T(8,128)(2,1)S(1)}, u32[]{:S(2)}, u32[]{:S(2)}) collective-permute-start(bf16[8,384,128]{2,1,0:T(8,128)(2,1)S(1)} %get-tuple-element.42), channel_id=1, source_target_pairs={{0,1},{1,0},{2,3},{3,2},{4,5},{5,4},{6,7},{7,6},{8,9},{9,8},{10,11... | collective-permute-start | bytes 2359304 | tf_op jit(solution)/shard_map/ppermute | solution.py:290
  14.0 15.1 %collective-permute-start.7 = (bf16[8,512,128]{2,1,0:T(8,128)(2,1)S(1)}, bf16[8,512,128]{2,1,0:T(8,128)(2,1)S(1)}, u32[]{:S(2)}, u32[]{:S(2)}) collective-permute-start(bf16[8,512,128]{2,1,0:T(8,128)(2,1)S(1)} %mm.17), channel_id=1, source_target_pairs={{0,1},{1,0},{2,3},{3,2},{4,5},{5,4},{6,7},{7,6},{8,9},{9,8},{10,11... | collective-permute-start | bytes 3145736 | tf_op jit(solution)/shard_map/ppermute | solution.py:290
  15.3 29.4 %collective-permute-start.1 = (bf16[8,512,128]{2,1,0:T(8,128)(2,1)S(1)}, bf16[8,512,128]{2,1,0:T(8,128)(2,1)S(1)}, u32[]{:S(2)}, u32[]{:S(2)}) collective-permute-start(bf16[8,512,128]{2,1,0:T(8,128)(2,1)S(1)} %mm.14), channel_id=1, source_target_pairs={{0,1},{1,0},{2,3},{3,2},{4,5},{5,4},{6,7},{7,6},{8,9},{9,8},{10,11... | collective-permute-start | bytes 3145736 | tf_op jit(solution)/shard_map/ppermute | solution.py:290
  24.1 20.4 %collective-permute-start.14 = (bf16[8,384,128]{2,1,0:T(8,128)(2,1)S(1)}, bf16[8,384,128]{2,1,0:T(8,128)(2,1)S(1)}, u32[]{:S(2)}, u32[]{:S(2)}) collective-permute-start(bf16[8,384,128]{2,1,0:T(8,128)(2,1)S(1)} %add_convert_fusion.3), channel_id=1, source_target_pairs={{2,4},{4,2},{6,0},{0,6},{3,5},{5,3},{7,1},{1,7},{10,12},{12,10},{1... | collective-permute-start | bytes 2359304 | tf_op jit(solution)/shard_map/ppermute | solution.py:290
  28.5 18.0 %collective-permute-start.18 = (bf16[8,400,128]{2,1,0:T(8,128)(2,1)S(1)}, bf16[8,400,128]{2,1,0:T(8,128)(2,1)S(1)}, u32[]{:S(2)}, u32[]{:S(2)}) collective-permute-start(bf16[8,400,128]{2,1,0:T(8,128)(2,1)S(1)} %get-tuple-element.45), channel_id=1, source_target_pairs={{0,1},{1,0},{2,3},{3,2},{4,5},{5,4},{6,7},{7,6},{8,9},{9,8},{10,11... | collective-permute-start | bytes 2457608 | tf_op jit(solution)/shard_map/ppermute | solution.py:290
  29.1 21.0 %collective-permute-start.20 = (bf16[8,400,128]{2,1,0:T(8,128)(2,1)S(1)}, bf16[8,400,128]{2,1,0:T(8,128)(2,1)S(1)}, u32[]{:S(2)}, u32[]{:S(2)}) collective-permute-start(bf16[8,400,128]{2,1,0:T(8,128)(2,1)S(1)} %add_convert_fusion.2), channel_id=1, source_target_pairs={{64,128},{128,64},{192,0},{0,192},{65,129},{129,65},{193,1},{1,193... | collective-permute-start | bytes 2457608 | tf_op jit(solution)/shard_map/ppermute | solution.py:290
  32.2 37.6 %collective-permute-start.6 = (bf16[8,512,128]{2,1,0:T(8,128)(2,1)S(1)}, bf16[8,512,128]{2,1,0:T(8,128)(2,1)S(1)}, u32[]{:S(2)}, u32[]{:S(2)}) collective-permute-start(bf16[8,512,128]{2,1,0:T(8,128)(2,1)S(1)} %get-tuple-element.39), channel_id=1, source_target_pairs={{0,1},{1,0},{2,3},{3,2},{4,5},{5,4},{6,7},{7,6},{8,9},{9,8},{10,11... | collective-permute-start | bytes 3145736 | tf_op jit(solution)/shard_map/ppermute | solution.py:290
  44.5 25.4 %collective-permute-start.8 = (bf16[8,512,128]{2,1,0:T(8,128)(2,1)S(1)}, bf16[8,512,128]{2,1,0:T(8,128)(2,1)S(1)}, u32[]{:S(2)}, u32[]{:S(2)}) collective-permute-start(bf16[8,512,128]{2,1,0:T(8,128)(2,1)S(1)} %add_convert_fusion), channel_id=1, source_target_pairs={{0,64},{64,0},{128,192},{192,128},{1,65},{65,1},{129,193},{193,129... | collective-permute-start | bytes 3145736 | tf_op jit(solution)/shard_map/ppermute | solution.py:290
  44.7 13.8 %collective-permute-start.15 = (bf16[4,384,128]{2,1,0:T(8,128)(2,1)S(1)}, bf16[4,384,128]{2,1,0:T(8,128)(2,1)S(1)}, u32[]{:S(2)}, u32[]{:S(2)}) collective-permute-start(bf16[4,384,128]{2,1,0:T(8,128)(2,1)S(1)} %add_convert_fusion.7), channel_id=1, source_target_pairs={{64,128},{128,64},{192,0},{0,192},{65,129},{129,65},{193,1},{1,193... | collective-permute-start | bytes 1179656 | tf_op jit(solution)/shard_map/ppermute | solution.py:290
  46.5 25.2 %collective-permute-start = (bf16[8,512,128]{2,1,0:T(8,128)(2,1)S(1)}, bf16[8,512,128]{2,1,0:T(8,128)(2,1)S(1)}, u32[]{:S(2)}, u32[]{:S(2)}) collective-permute-start(bf16[8,512,128]{2,1,0:T(8,128)(2,1)S(1)} %get-tuple-element.36), channel_id=1, source_target_pairs={{0,1},{1,0},{2,3},{3,2},{4,5},{5,4},{6,7},{7,6},{8,9},{9,8},{10,11... | collective-permute-start | bytes 3145736 | tf_op jit(solution)/shard_map/ppermute | solution.py:290
  50.1 23.0 %collective-permute-start.2 = (bf16[8,512,128]{2,1,0:T(8,128)(2,1)S(1)}, bf16[8,512,128]{2,1,0:T(8,128)(2,1)S(1)}, u32[]{:S(2)}, u32[]{:S(2)}) collective-permute-start(bf16[8,512,128]{2,1,0:T(8,128)(2,1)S(1)} %add_convert_fusion.1), channel_id=1, source_target_pairs={{0,2},{2,0},{4,6},{6,4},{1,3},{3,1},{5,7},{7,5},{8,10},{10,8},{12,... | collective-permute-start | bytes 3145736 | tf_op jit(solution)/shard_map/ppermute | solution.py:290
  58.5 11.2 %collective-permute-start.21 = (bf16[4,400,128]{2,1,0:T(8,128)(2,1)S(1)}, bf16[4,400,128]{2,1,0:T(8,128)(2,1)S(1)}, u32[]{:S(2)}, u32[]{:S(2)}) collective-permute-start(bf16[4,400,128]{2,1,0:T(8,128)(2,1)S(1)} %add_convert_fusion.6), channel_id=1, source_target_pairs={{2,4},{4,2},{6,0},{0,6},{3,5},{5,3},{7,1},{1,7},{10,12},{12,10},{1... | collective-permute-start | bytes 1228808 | tf_op jit(solution)/shard_map/ppermute | solution.py:290
  69.7 7.6 %collective-permute-start.16 = (bf16[2,384,128]{2,1,0:T(8,128)(2,1)S(1)}, bf16[2,384,128]{2,1,0:T(8,128)(2,1)S(1)}, u32[]{:S(2)}, u32[]{:S(2)}) collective-permute-start(bf16[2,384,128]{2,1,0:T(8,128)(2,1)S(1)} %add_convert_fusion.11), channel_id=1, source_target_pairs={{0,2},{2,0},{4,6},{6,4},{1,3},{3,1},{5,7},{7,5},{8,10},{10,8},{12,... | collective-permute-start | bytes 589832 | tf_op jit(solution)/shard_map/ppermute | solution.py:290
  69.8 7.7 %collective-permute-start.22 = (bf16[2,400,128]{2,1,0:T(8,128)(2,1)S(1)}, bf16[2,400,128]{2,1,0:T(8,128)(2,1)S(1)}, u32[]{:S(2)}, u32[]{:S(2)}) collective-permute-start(bf16[2,400,128]{2,1,0:T(8,128)(2,1)S(1)} %add_convert_fusion.10), channel_id=1, source_target_pairs={{0,64},{64,0},{128,192},{192,128},{1,65},{65,1},{129,193},{193,129... | collective-permute-start | bytes 614408 | tf_op jit(solution)/shard_map/ppermute | solution.py:290
  70.2 18.4 %collective-permute-start.9 = (bf16[4,512,128]{2,1,0:T(8,128)(2,1)S(1)}, bf16[4,512,128]{2,1,0:T(8,128)(2,1)S(1)}, u32[]{:S(2)}, u32[]{:S(2)}) collective-permute-start(bf16[4,512,128]{2,1,0:T(8,128)(2,1)S(1)} %add_convert_fusion.4), channel_id=1, source_target_pairs={{0,2},{2,0},{4,6},{6,4},{1,3},{3,1},{5,7},{7,5},{8,10},{10,8},{12,... | collective-permute-start | bytes 1572872 | tf_op jit(solution)/shard_map/ppermute | solution.py:290
  73.3 17.2 %collective-permute-start.3 = (bf16[4,512,128]{2,1,0:T(8,128)(2,1)S(1)}, bf16[4,512,128]{2,1,0:T(8,128)(2,1)S(1)}, u32[]{:S(2)}, u32[]{:S(2)}) collective-permute-start(bf16[4,512,128]{2,1,0:T(8,128)(2,1)S(1)} %add_convert_fusion.5), channel_id=1, source_target_pairs={{0,64},{64,0},{128,192},{192,128},{1,65},{65,1},{129,193},{193,129... | collective-permute-start | bytes 1572872 | tf_op jit(solution)/shard_map/ppermute | solution.py:290
  77.4 9.0 %collective-permute-start.17 = (bf16[1,384,128]{2,1,0:T(8,128)(2,1)S(1)}, bf16[1,384,128]{2,1,0:T(8,128)(2,1)S(1)}, u32[]{:S(2)}, u32[]{:S(2)}) collective-permute-start(bf16[1,384,128]{2,1,0:T(8,128)(2,1)S(1)} %add_convert_fusion.15), channel_id=1, source_target_pairs={{0,64},{64,0},{128,192},{192,128},{1,65},{65,1},{129,193},{193,129... | collective-permute-start | bytes 294920 | tf_op jit(solution)/shard_map/ppermute | solution.py:290
  77.6 14.2 %collective-permute-start.23 = (bf16[1,400,128]{2,1,0:T(8,128)(2,1)S(1)}, bf16[1,400,128]{2,1,0:T(8,128)(2,1)S(1)}, u32[]{:S(2)}, u32[]{:S(2)}) collective-permute-start(bf16[1,400,128]{2,1,0:T(8,128)(2,1)S(1)} %add_convert_fusion.14), channel_id=1, source_target_pairs={{0,2},{2,0},{4,6},{6,4},{1,3},{3,1},{5,7},{7,5},{8,10},{10,8},{12,... | collective-permute-start | bytes 307208 | tf_op jit(solution)/shard_map/ppermute | solution.py:290
  88.7 6.5 %collective-permute-start.10 = (bf16[2,512,128]{2,1,0:T(8,128)(2,1)S(1)}, bf16[2,512,128]{2,1,0:T(8,128)(2,1)S(1)}, u32[]{:S(2)}, u32[]{:S(2)}) collective-permute-start(bf16[2,512,128]{2,1,0:T(8,128)(2,1)S(1)} %add_convert_fusion.8), channel_id=1, source_target_pairs={{2,4},{4,2},{6,0},{0,6},{3,5},{5,3},{7,1},{1,7},{10,12},{12,10},{1... | collective-permute-start | bytes 786440 | tf_op jit(solution)/shard_map/ppermute | solution.py:290
  90.7 12.8 %copy-start.3 = (s32[1,179]{1,0:T(1,128)S(1)}, s32[1,179]{1,0:T(1,128)}, u32[]{:S(2)}) copy-start(s32[1,179]{1,0:T(1,128)} %ids_ref.1) | copy-start | bytes 2152
  90.7 12.8 %copy-start.4 = (s32[14,1]{0,1:T(1,128)S(1)}, s32[14,1]{0,1:T(1,128)}, u32[]{:S(2)}) copy-start(s32[14,1]{0,1:T(1,128)} %param.12) | copy-start | bytes 172
  90.7 7.2 %collective-permute-start.4 = (bf16[2,512,128]{2,1,0:T(8,128)(2,1)S(1)}, bf16[2,512,128]{2,1,0:T(8,128)(2,1)S(1)}, u32[]{:S(2)}, u32[]{:S(2)}) collective-permute-start(bf16[2,512,128]{2,1,0:T(8,128)(2,1)S(1)} %add_convert_fusion.9), channel_id=1, source_target_pairs={{64,128},{128,64},{192,0},{0,192},{65,129},{129,65},{193,1},{1,193... | collective-permute-start | bytes 786440 | tf_op jit(solution)/shard_map/ppermute | solution.py:290
  95.3 9.6 %copy-start = (f32[179,128]{1,0:T(8,128)S(1)}, f32[179,128]{1,0:T(8,128)}, u32[]{:S(2)}) copy-start(f32[179,128]{1,0:T(8,128)} %ma_ref.1) | copy-start | bytes 274948
  95.3 9.6 %copy-start.1 = (f32[179,128]{1,0:T(8,128)S(1)}, f32[179,128]{1,0:T(8,128)}, u32[]{:S(2)}) copy-start(f32[179,128]{1,0:T(8,128)} %mo_ref.1) | copy-start | bytes 274948
  95.4 9.6 %copy-start.2 = (f32[179,128]{1,0:T(8,128)S(1)}, f32[179,128]{1,0:T(8,128)}, u32[]{:S(2)}) copy-start(f32[179,128]{1,0:T(8,128)} %se_ref.1) | copy-start | bytes 274948
  95.4 6.8 %collective-permute-start.11 = (bf16[1,512,128]{2,1,0:T(8,128)(2,1)S(1)}, bf16[1,512,128]{2,1,0:T(8,128)(2,1)S(1)}, u32[]{:S(2)}, u32[]{:S(2)}) collective-permute-start(bf16[1,512,128]{2,1,0:T(8,128)(2,1)S(1)} %add_convert_fusion.12), channel_id=1, source_target_pairs={{64,128},{128,64},{192,0},{0,192},{65,129},{129,65},{193,1},{1,193... | collective-permute-start | bytes 393224 | tf_op jit(solution)/shard_map/ppermute | solution.py:290
  98.0 5.4 %collective-permute-start.5 = (bf16[1,512,128]{2,1,0:T(8,128)(2,1)S(1)}, bf16[1,512,128]{2,1,0:T(8,128)(2,1)S(1)}, u32[]{:S(2)}, u32[]{:S(2)}) collective-permute-start(bf16[1,512,128]{2,1,0:T(8,128)(2,1)S(1)} %add_convert_fusion.13), channel_id=1, source_target_pairs={{2,4},{4,2},{6,0},{0,6},{3,5},{5,3},{7,1},{1,7},{10,12},{12,10},{1... | collective-permute-start | bytes 393224 | tf_op jit(solution)/shard_map/ppermute | solution.py:290
  105.7 7.6 %collective-permute-start.24 = (bf16[179,128]{1,0:T(8,128)(2,1)S(1)}, bf16[179,128]{1,0:T(8,128)(2,1)S(1)}, u32[]{:S(2)}, u32[]{:S(2)}) collective-permute-start(bf16[179,128]{1,0:T(8,128)(2,1)S(1)} %get-tuple-element.50.a_ref), channel_id=1, source_target_pairs={{0,1},{1,0},{2,3},{3,2},{4,5},{5,4},{6,7},{7,6},{8,9},{9,8},{10,11... | collective-permute-start | bytes 137480 | tf_op jit(solution)/shard_map/ppermute | solution.py:290
  113.4 7.9 %collective-permute-start.25 = (bf16[2,179,128]{2,1,0:T(8,128)(2,1)S(1)}, bf16[2,179,128]{2,1,0:T(8,128)(2,1)S(1)}, u32[]{:S(2)}, u32[]{:S(2)}) collective-permute-start(bf16[2,179,128]{2,1,0:T(8,128)(2,1)S(1)} %pad_maximum_fusion.1), channel_id=1, source_target_pairs={{0,2},{2,0},{4,6},{6,4},{1,3},{3,1},{5,7},{7,5},{8,10},{10,8},{12,... | collective-permute-start | bytes 274952 | tf_op jit(solution)/shard_map/ppermute | solution.py:290
  113.5 11.8 %collective-permute-start.27 = (bf16[4,128,128]{2,1,0:T(8,128)(2,1)S(1)}, bf16[4,128,128]{2,1,0:T(8,128)(2,1)S(1)}, u32[]{:S(2)}, u32[]{:S(2)}) collective-permute-start(bf16[4,128,128]{2,1,0:T(8,128)(2,1)S(1)} %get-tuple-element.52), channel_id=1, source_target_pairs={{0,8},{8,16},{16,24},{24,32},{32,40},{40,48},{48,56},{56,0},{1,9},... | collective-permute-start | bytes 393224 | tf_op jit(solution)/shard_map/ppermute | solution.py:290
  114.5 13.3 %collective-permute-start.28 = (bf16[4,128,128]{2,1,0:T(8,128)(2,1)S(1)}, bf16[4,128,128]{2,1,0:T(8,128)(2,1)S(1)}, u32[]{:S(2)}, u32[]{:S(2)}) collective-permute-start(bf16[4,128,128]{2,1,0:T(8,128)(2,1)S(1)} %get-tuple-element.53), channel_id=1, source_target_pairs={{0,16},{8,24},{16,32},{24,40},{32,48},{40,56},{48,0},{56,8},{1,17}... | collective-permute-start | bytes 393224 | tf_op jit(solution)/shard_map/ppermute | solution.py:290
  117.5 20.4 %collective-permute-start.29 = (bf16[4,128,128]{2,1,0:T(8,128)(2,1)S(1)}, bf16[4,128,128]{2,1,0:T(8,128)(2,1)S(1)}, u32[]{:S(2)}, u32[]{:S(2)}) collective-permute-start(bf16[4,128,128]{2,1,0:T(8,128)(2,1)S(1)} %get-tuple-element.54), channel_id=1, source_target_pairs={{0,24},{8,32},{16,40},{24,48},{32,56},{40,0},{48,8},{56,16},{1,25}... | collective-permute-start | bytes 393224 | tf_op jit(solution)/shard_map/ppermute | solution.py:290
  121.3 27.5 %collective-permute-start.26 = (bf16[4,179,128]{2,1,0:T(8,128)(2,1)S(1)}, bf16[4,179,128]{2,1,0:T(8,128)(2,1)S(1)}, u32[]{:S(2)}, u32[]{:S(2)}) collective-permute-start(bf16[4,179,128]{2,1,0:T(8,128)(2,1)S(1)} %pad_maximum_fusion), channel_id=1, source_target_pairs={{2,4},{4,2},{6,0},{0,6},{3,5},{5,3},{7,1},{1,7},{10,12},{12,10},{1... | collective-permute-start | bytes 549896 | tf_op jit(solution)/shard_map/ppermute | solution.py:290
  122.9 15.6 %collective-permute-start.30 = (bf16[4,128,128]{2,1,0:T(8,128)(2,1)S(1)}, bf16[4,128,128]{2,1,0:T(8,128)(2,1)S(1)}, u32[]{:S(2)}, u32[]{:S(2)}) collective-permute-start(bf16[4,128,128]{2,1,0:T(8,128)(2,1)S(1)} %get-tuple-element.55), channel_id=1, source_target_pairs={{0,32},{8,40},{16,48},{24,56},{32,0},{40,8},{48,16},{56,24},{1,33}... | collective-permute-start | bytes 393224 | tf_op jit(solution)/shard_map/ppermute | solution.py:290
  125.3 15.1 %collective-permute-start.31 = (bf16[4,128,128]{2,1,0:T(8,128)(2,1)S(1)}, bf16[4,128,128]{2,1,0:T(8,128)(2,1)S(1)}, u32[]{:S(2)}, u32[]{:S(2)}) collective-permute-start(bf16[4,128,128]{2,1,0:T(8,128)(2,1)S(1)} %get-tuple-element.56), channel_id=1, source_target_pairs={{0,40},{8,48},{16,56},{24,0},{32,8},{40,16},{48,24},{56,32},{1,41}... | collective-permute-start | bytes 393224 | tf_op jit(solution)/shard_map/ppermute | solution.py:290
  127.9 20.0 %collective-permute-start.32 = (bf16[4,128,128]{2,1,0:T(8,128)(2,1)S(1)}, bf16[4,128,128]{2,1,0:T(8,128)(2,1)S(1)}, u32[]{:S(2)}, u32[]{:S(2)}) collective-permute-start(bf16[4,128,128]{2,1,0:T(8,128)(2,1)S(1)} %get-tuple-element.57), channel_id=1, source_target_pairs={{0,48},{8,56},{16,0},{24,8},{32,16},{40,24},{48,32},{56,40},{1,49}... | collective-permute-start | bytes 393224 | tf_op jit(solution)/shard_map/ppermute | solution.py:290
  137.9 10.8 %collective-permute-start.33 = (bf16[4,128,128]{2,1,0:T(8,128)(2,1)S(1)}, bf16[4,128,128]{2,1,0:T(8,128)(2,1)S(1)}, u32[]{:S(2)}, u32[]{:S(2)}) collective-permute-start(bf16[4,128,128]{2,1,0:T(8,128)(2,1)S(1)} %get-tuple-element.58), channel_id=1, source_target_pairs={{0,56},{8,0},{16,8},{24,16},{32,24},{40,32},{48,40},{56,48},{1,57}... | collective-permute-start | bytes 393224 | tf_op jit(solution)/shard_map/ppermute | solution.py:290
